TPU v7x, 32 devices: a whole 2x2x4 slice. The times are simulated.
32 devices in a mesh: ep: 32 (over z, y, x, core).
Axes of the slice: x: 2, y: 2, z: 4, core: 2. Of those that a mesh axis runs over, the one named last changes fastest.
Arguments:
- hidden: bfloat16 [2, 1024, 3584], P(None, 'ep'), may hold values from -6 to 6
- expert_ids: int32 [2, 1024, 8], P(None, 'ep'), may hold values from 0 to 31, all different within a row; in each aligned block of 32 rows (0 to 31, 32 to 63, ..., all dimensions but the last counted through in order) at most 9 rows name the same one
- gate_scores: float32 [2, 1024, 8], P(None, 'ep'), may hold values from 0.05 to 1
- w_gate: bfloat16 [32, 3584, 1024], P('ep'), may hold values from -0.09375 to 0.09375
- w_up: bfloat16 [32, 3584, 1024], P('ep'), may hold values from -0.09375 to 0.09375
- w_down: bfloat16 [32, 1024, 3584], P('ep'), may hold values from -0.1875 to 0.1875
Outputs:
- mixed: bfloat16 [2, 1024, 3584], P(None, 'ep')
- expert_load: float32 [32], P('ep')
Inputs may be any that keep to these rules, and one draw needn't show every extreme that they name: `expert_ids`: among the 32 rows of one device in one micro-batch, no expert is named by more than 9 rows, a bound that some block reaches. Each row names 8 different experts.
All inputs are finite; a program needn't handle non-finite values.
Results may differ from a plain program's by a relative error of at most 0.004.
The roundings to bfloat16 on the way count: a program that leaves them out, or rounds other values in their place, can miss the bound.
Values may be sent and summed in bfloat16 or wider, within the bound.
A program may use at most 128 MiB of HBM per device.

v0:
```python
import functools

import jax
import jax.numpy as jnp
from jax import lax
from jax.experimental import pallas as pl
from jax.experimental.pallas import tpu as pltpu
from jax.sharding import PartitionSpec as P

route_scale = 2.5
PLANE = 8
MESH = pl.DeviceIdType.MESH


def gather_kernel(
    planes,
    capacity,
    chosen,
    x_ref,
    g_ref,
    rows_ref,
    notes_ref,
    table,
    local_sem,
    recv_sem,
    core_recv,
    up_sem,
    down_sem,
    x_sem,
    y_sem,
    core_sem,
    table_sem,
):
    me = lax.axis_index("ep")
    p = me // PLANE
    quad = (me % PLANE) // 2
    core = me % 2
    x_quad = quad + 1 - 2 * (quad % 2)
    y_quad = (quad + 2) % 4
    d_quad = 3 - quad

    def dev(at_plane, at_quad, at_core=core):
        return at_plane * PLANE + at_quad * 2 + at_core

    def block(at_plane, at_quad, at_core=core):
        return g_ref.at[at_quad * 2 + at_core, at_plane]

    up, down = me + PLANE, me - PLANE
    x_dev, y_dev, c_dev = dev(p, x_quad), dev(p, y_quad), dev(p, quad, 1 - core)

    barrier = pltpu.get_barrier_semaphore()
    for other in (x_dev, y_dev, c_dev):
        pl.semaphore_signal(barrier, inc=1, device_id=(other,), device_id_type=MESH)

    @pl.when(p < planes - 1)
    def _():
        pl.semaphore_signal(barrier, inc=1, device_id=(up,), device_id_type=MESH)

    @pl.when(p > 0)
    def _():
        pl.semaphore_signal(barrier, inc=1, device_id=(down,), device_id_type=MESH)

    below = (p + planes - 1) // planes
    above = (2 * planes - 2 - p) // planes
    pl.semaphore_wait(barrier, 3 + below + above)

    local = pltpu.make_async_copy(x_ref, block(p, quad), local_sem)
    local.start()

    def half(at_plane, at_quad, m, send_sem, to, own=False):
        place = block(at_plane, at_quad).at[m]
        return pltpu.make_async_remote_copy(
            src_ref=x_ref.at[m] if own else place,
            dst_ref=place,
            send_sem=send_sem,
            recv_sem=recv_sem.at[at_plane, at_quad, m],
            device_id=(to,),
            device_id_type=MESH,
        )

    def to_up(at_plane, m, own=False):
        return half(at_plane, quad, m, up_sem.at[at_plane, m], up, own)

    def to_down(at_plane, m, own=False):
        return half(at_plane, quad, m, down_sem.at[at_plane, m], down, own)

    def to_x(at_plane, m, own=False):
        return half(at_plane, quad, m, x_sem.at[at_plane, m], x_dev, own)

    def to_y(at_plane, m, own=False):
        return half(at_plane, quad, m, y_sem.at[at_plane, m], y_dev, own)

    def on_y(at_plane):
        return half(at_plane, x_quad, 0, y_sem.at[at_plane, 2], y_dev)

    def on_x(at_plane):
        return half(at_plane, y_quad, 1, x_sem.at[at_plane, 2], x_dev)

    def arrived(at_plane, at_quad, m):
        half(at_plane, at_quad, m, x_sem.at[at_plane, 0], x_dev).wait_recv()

    def to_core(at_plane, at_quad, own=False):
        place = block(at_plane, at_quad)
        return pltpu.make_async_remote_copy(
            src_ref=x_ref if own else place,
            dst_ref=place,
            send_sem=core_sem.at[at_plane, at_quad],
            recv_sem=core_recv.at[at_plane, at_quad],
            device_id=(c_dev,),
            device_id_type=MESH,
        )

    def core_arrived(at_plane, at_quad):
        place = block(at_plane, at_quad, 1 - core)
        pltpu.make_async_remote_copy(
            src_ref=place,
            dst_ref=place,
            send_sem=core_sem.at[at_plane, at_quad],
            recv_sem=core_recv.at[at_plane, at_quad],
            device_id=(c_dev,),
            device_id_type=MESH,
        ).wait_recv()

    for m in range(2):

        @pl.when(p < planes - 1)
        def _():
            to_up(p, m, True).start()

        @pl.when(p > 0)
        def _():
            to_down(p, m, True).start()

        to_x(p, m, True).start()
        to_y(p, m, True).start()
    to_core(p, quad, True).start()

    for s in range(1, planes):

        @pl.when(p >= s)
        def _():
            for m in range(2):
                arrived(p - s, quad, m)

                @pl.when(p < planes - 1)
                def _():
                    to_up(p - s, m).start()

                to_x(p - s, m).start()
                to_y(p - s, m).start()
            to_core(p - s, quad).start()

        @pl.when(p + s < planes)
        def _():
            for m in range(2):
                arrived(p + s, quad, m)

                @pl.when(p > 0)
                def _():
                    to_down(p + s, m).start()

                to_x(p + s, m).start()
                to_y(p + s, m).start()
            to_core(p + s, quad).start()

    def each(body):
        body(p)
        for s in range(1, planes):
            pl.when(p >= s)(functools.partial(body, p - s))
            pl.when(p + s < planes)(functools.partial(body, p + s))

    def across(at):
        arrived(at, x_quad, 0)
        on_y(at).start()
        arrived(at, y_quad, 0)
        arrived(at, y_quad, 1)
        on_x(at).start()
        arrived(at, x_quad, 1)
        to_core(at, x_quad).start()
        to_core(at, y_quad).start()

    def diagonal(at):
        arrived(at, d_quad, 0)
        arrived(at, d_quad, 1)
        to_core(at, d_quad).start()

    local.wait()

    tok_mb, wide = x_ref.shape[1:]
    depth = planes * 2 * tok_mb
    model_width = rows_ref.shape[2]
    token = lax.broadcasted_iota(jnp.int32, (depth, depth), 0)
    other = lax.broadcasted_iota(jnp.int32, (depth, depth), 1)
    before = (other < token) & (lax.div(other, tok_mb) == lax.div(token, tok_mb))
    before = jnp.where(before, 1.0, 0.0).astype(jnp.bfloat16)
    lanes = (depth, 128)
    start = lax.div(lax.broadcasted_iota(jnp.int32, lanes, 0), tok_mb) * capacity
    lane = lax.broadcasted_iota(jnp.int32, lanes, 1)

    def fetch(place, slot):
        return pltpu.make_async_copy(g_ref.at[place], table.at[slot], table_sem.at[slot])

    def select(place, slot):
        fetch(place, slot).wait()
        notes = table[slot, :, :, :, model_width:]
        notes_ref[place] = notes
        ids = notes.reshape(lanes).astype(jnp.float32).astype(jnp.int32)
        named = jnp.where((ids == me) & (lane < chosen), 1.0, 0.0)
        named = jnp.broadcast_to(jnp.sum(named, axis=1, keepdims=True), lanes)
        rank = jnp.dot(before, named.astype(jnp.bfloat16), preferred_element_type=jnp.float32)
        spot = start + rank.astype(jnp.int32)
        pick = jnp.where((lane == spot) & (named > 0.5), 1.0, 0.0).astype(jnp.bfloat16)
        found = lax.dot_general(
            pick,
            table[slot, :, :, :, :model_width].reshape(depth, model_width),
            (((0,), (0,)), ((), ())),
            preferred_element_type=jnp.float32,
        )
        rows_ref[place] = found[: rows_ref.shape[1]].astype(jnp.bfloat16)

    each(across)

    def others(at_quad):
        each(lambda at: core_arrived(at, at_quad))

    fetch(quad * 2 + core, 0).start()
    fetch(x_quad * 2 + core, 1).start()
    select(quad * 2 + core, 0)
    fetch(y_quad * 2 + core, 0).start()
    select(x_quad * 2 + core, 1)
    others(quad)
    fetch(quad * 2 + 1 - core, 1).start()
    select(y_quad * 2 + core, 0)
    others(x_quad)
    fetch(x_quad * 2 + 1 - core, 0).start()
    select(quad * 2 + 1 - core, 1)
    each(diagonal)
    fetch(d_quad * 2 + core, 1).start()
    select(x_quad * 2 + 1 - core, 0)
    others(y_quad)
    fetch(y_quad * 2 + 1 - core, 0).start()
    select(d_quad * 2 + core, 1)
    others(d_quad)
    fetch(d_quad * 2 + 1 - core, 1).start()
    select(y_quad * 2 + 1 - core, 0)
    select(d_quad * 2 + 1 - core, 1)

    def finish(at):
        for at_quad in (quad, x_quad, y_quad, d_quad):
            to_core(at, at_quad).wait_send()
        for m in range(2):
            to_x(at, m).wait_send()
            to_y(at, m).wait_send()
        on_x(at).wait_send()
        on_y(at).wait_send()

    each(finish)
    for s in range(planes):

        @pl.when((p >= s) & (p < planes - 1))
        def _():
            for m in range(2):
                to_up(p - s, m).wait_send()

        @pl.when((p + s < planes) & (p > 0))
        def _():
            for m in range(2):
                to_down(p + s, m).wait_send()


def gather_all(x, model_width, capacity, chosen, devices):
    planes = devices // PLANE
    dma = pltpu.SemaphoreType.DMA
    return pl.pallas_call(
        functools.partial(gather_kernel, planes, capacity, chosen),
        out_shape=(
            jax.ShapeDtypeStruct((PLANE, planes) + x.shape, x.dtype),
            jax.ShapeDtypeStruct((PLANE, planes * 2 * capacity, model_width), x.dtype),
            jax.ShapeDtypeStruct((PLANE, planes) + x.shape[:2] + (128,), x.dtype),
        ),
        in_specs=[pl.BlockSpec(memory_space=pltpu.VMEM)],
        out_specs=(
            pl.BlockSpec(memory_space=pl.ANY),
            pl.BlockSpec(memory_space=pltpu.VMEM),
            pl.BlockSpec(memory_space=pltpu.VMEM),
        ),
        scratch_shapes=[
            pltpu.VMEM((2, planes) + x.shape, x.dtype),
            dma,
            dma((planes, 4, 2)),
            dma((planes, 4)),
            dma((planes, 2)),
            dma((planes, 2)),
            dma((planes, 3)),
            dma((planes, 3)),
            dma((planes, 4)),
            dma((2,)),
        ],
        compiler_params=pltpu.CompilerParams(collective_id=0, has_side_effects=True),
    )(x)


def return_kernel(
    planes, hid_ref, down_ref, matrix_ref, out_ref, w_buf, answers, inbox, sums, column, w_sem, a_send, a_recv, s_send, s_recv
):
    me = lax.axis_index("ep")
    p = me // PLANE
    q = me % PLANE
    chunks, depth, width = w_buf.shape

    def load(c):
        place = pl.multiple_of(c * width, width)
        return pltpu.make_async_copy(
            down_ref.at[:, pl.ds(place, width)], w_buf.at[c], w_sem.at[c]
        )

    for c in range(chunks):
        load(c).start()

    barrier = pltpu.get_barrier_semaphore()
    for i in range(1, PLANE):
        other = p * PLANE + (q + i) % PLANE
        pl.semaphore_signal(barrier, inc=1, device_id=(other,), device_id_type=MESH)
    for i in range(1, planes):
        other = ((p + i) % planes) * PLANE + q
        pl.semaphore_signal(barrier, inc=1, device_id=(other,), device_id_type=MESH)
    pl.semaphore_wait(barrier, PLANE + planes - 2)

    def answer_copy(c, i):
        place = (q + i) % PLANE
        return pltpu.make_async_remote_copy(
            src_ref=answers.at[c, place],
            dst_ref=inbox.at[c, q],
            send_sem=a_send.at[c, i],
            recv_sem=a_recv.at[c, q],
            device_id=(p * PLANE + place,),
            device_id_type=MESH,
        )

    def answer_arrived(c, i):
        place = (q + i) % PLANE
        pltpu.make_async_remote_copy(
            src_ref=answers.at[c, place],
            dst_ref=inbox.at[c, place],
            send_sem=a_send.at[c, i],
            recv_sem=a_recv.at[c, place],
            device_id=(p * PLANE + place,),
            device_id_type=MESH,
        ).wait_recv()

    def sum_copy(c, i):
        place = (p + i) % planes
        return pltpu.make_async_remote_copy(
            src_ref=sums.at[c, place],
            dst_ref=column.at[c, p],
            send_sem=s_send.at[c, i],
            recv_sem=s_recv.at[c, p],
            device_id=(place * PLANE + q,),
            device_id_type=MESH,
        )

    def sum_arrived(c, i):
        place = (p + i) % planes
        pltpu.make_async_remote_copy(
            src_ref=sums.at[c, place],
            dst_ref=column.at[c, place],
            send_sem=s_send.at[c, i],
            recv_sem=s_recv.at[c, place],
            device_id=(place * PLANE + q,),
            device_id_type=MESH,
        ).wait_recv()

    def compute(c, carry):
        load(c).wait()
        found = jnp.dot(hid_ref[...], w_buf[c], preferred_element_type=jnp.float32)
        answers[c] = found.reshape(answers.shape[1:]).astype(jnp.bfloat16)
        for i in range(1, PLANE):
            answer_copy(c, i).start()
        inbox[c, q] = answers[c, q]
        return carry

    lax.fori_loop(0, chunks, compute, 0)

    def combine(c, carry):
        for i in range(1, PLANE):
            answer_arrived(c, i)
        total = jnp.zeros((matrix_ref.shape[2], width), jnp.float32)
        for k in range(PLANE):
            for half in range(2):
                total += jnp.dot(
                    matrix_ref[k, half], inbox[c, k], preferred_element_type=jnp.float32
                )
        sums[c] = total.reshape(sums.shape[1:]).astype(jnp.bfloat16)
        for i in range(1, planes):
            sum_copy(c, i).start()
        column[c, p] = sums[c, p]
        return carry

    lax.fori_loop(0, chunks, combine, 0)

    def gather_sums(c, carry):
        for i in range(1, planes):
            sum_arrived(c, i)
        total = column[c, 0].astype(jnp.float32)
        for k in range(1, planes):
            total += column[c, k].astype(jnp.float32)
        out_ref[c] = total.astype(jnp.bfloat16)
        return carry

    lax.fori_loop(0, chunks, gather_sums, 0)

    def finish(c, carry):
        for i in range(1, PLANE):
            answer_copy(c, i).wait_send()
        for i in range(1, planes):
            sum_copy(c, i).wait_send()
        return carry

    lax.fori_loop(0, chunks, finish, 0)


def return_all(hid, w_down, matrix, devices):
    planes = devices // PLANE
    depth, model_width = w_down.shape
    width = next(w for w in (512, 256, 128) if model_width % w == 0)
    chunks = model_width // width
    rows = hid.shape[0] // PLANE
    tokens = matrix.shape[2] // planes
    dma = pltpu.SemaphoreType.DMA
    vmem = pl.BlockSpec(memory_space=pltpu.VMEM)
    return pl.pallas_call(
        functools.partial(return_kernel, planes),
        out_shape=jax.ShapeDtypeStruct((chunks, tokens, width), jnp.bfloat16),
        in_specs=[vmem, pl.BlockSpec(memory_space=pl.ANY), vmem],
        out_specs=vmem,
        scratch_shapes=[
            pltpu.VMEM((chunks, depth, width), jnp.bfloat16),
            pltpu.VMEM((chunks, PLANE, rows, width), jnp.bfloat16),
            pltpu.VMEM((chunks, PLANE, rows, width), jnp.bfloat16),
            pltpu.VMEM((chunks, planes, tokens, width), jnp.bfloat16),
            pltpu.VMEM((chunks, planes, tokens, width), jnp.bfloat16),
            dma((chunks,)),
            dma((chunks, PLANE)),
            dma((chunks, PLANE)),
            dma((chunks, planes)),
            dma((chunks, planes)),
        ],
        compiler_params=pltpu.CompilerParams(collective_id=1, has_side_effects=True),
    )(hid, w_down, matrix)


def parts_of(values, count):
    parts = []
    for _ in range(count):
        part = lax.reduce_precision(values, 8, 7)
        parts.append(part.astype(jnp.bfloat16))
        values = values - part
    return parts


def ranks(mask):
    rows = mask.shape[-1]
    earlier = (jnp.arange(rows)[:, None] < jnp.arange(rows)[None, :]).astype(jnp.bfloat16)
    found = jnp.einsum(
        "...r,rt->...t", mask.astype(jnp.bfloat16), earlier, preferred_element_type=jnp.float32
    )
    return found.astype(jnp.int32)


def shards(hidden, expert_ids, gate_scores, w_gate, w_up, w_down):
    devices = lax.axis_size("ep")
    planes = devices // PLANE
    me = lax.axis_index("ep")
    my_plane, my_place = me // PLANE, me % PLANE
    micro_count, tok_mb, model_width = hidden.shape
    chosen = expert_ids.shape[2]
    capacity = tok_mb * chosen // devices + 1
    weights = route_scale * gate_scores / jnp.sum(gate_scores, axis=-1, keepdims=True)

    extra = jnp.concatenate([expert_ids.astype(jnp.bfloat16)] + parts_of(weights, 3), axis=-1)
    extra = jnp.pad(extra, ((0, 0), (0, 0), (0, 128 - extra.shape[-1])))
    _, rows, notes = gather_all(
        jnp.concatenate([hidden, extra], axis=-1), model_width, capacity, chosen, devices
    )
    rows = rows.reshape(-1, model_width)
    notes = notes.astype(jnp.float32)
    all_ids = notes[..., :chosen].astype(jnp.int32)
    all_weights = (
        notes[..., chosen : 2 * chosen]
        + notes[..., 2 * chosen : 3 * chosen]
        + notes[..., 3 * chosen : 4 * chosen]
    )
    named = all_ids == me
    expert_load = jnp.sum(jnp.where(named, all_weights, 0.0)).reshape(1) * (
        devices / (route_scale * micro_count * tok_mb * devices)
    )

    slots = jnp.arange(capacity, dtype=jnp.int32)
    gate = jnp.dot(rows, w_gate[0], preferred_element_type=jnp.float32)
    upper = jnp.dot(rows, w_up[0], preferred_element_type=jnp.float32)
    hid = (jax.nn.silu(gate) * upper).astype(jnp.bfloat16)

    ids = lax.dynamic_index_in_dim(all_ids, my_place, 0, keepdims=False)
    share = lax.dynamic_index_in_dim(all_weights, my_place, 0, keepdims=False)
    experts_here = my_plane * PLANE + jnp.arange(PLANE, dtype=jnp.int32)
    same = ids[:, :, None] == experts_here[:, None, None]
    here = jnp.any(same, axis=-1)
    weight_here = jnp.sum(jnp.where(same, share[:, :, None], 0.0), axis=-1)
    spots = here[..., None] & (ranks(here)[..., None] == slots)
    spread = jnp.where(spots, weight_here[..., None], 0.0)
    groups = planes * micro_count
    spread = spread.transpose(2, 0, 1, 3, 4).reshape(PLANE, groups, tok_mb, 1, capacity)
    diag = jnp.eye(groups, dtype=jnp.float32)[:, None, :, None]
    matrix = (spread * diag).reshape(PLANE, groups * tok_mb, groups * capacity)
    matrix = jnp.stack(parts_of(matrix, 2), axis=1)
    mixed = return_all(hid, w_down[0], matrix, devices)
    mixed = mixed.transpose(1, 0, 2)
    return (mixed.reshape(micro_count, tok_mb, model_width), expert_load)


def solution(mesh):
    placed = (
        P(None, "ep", None),
        P(None, "ep", None),
        P(None, "ep", None),
        P("ep", None, None),
        P("ep", None, None),
        P("ep", None, None),
    )
    return jax.shard_map(
        shards,
        mesh=mesh,
        in_specs=placed,
        out_specs=(P(None, "ep", None), P("ep")),
        check_vma=False,
    )
```

profile of v0, /device:TPU:0, one launch (start us, length us, event | category | flops | bytes accessed | tf_op | source)
XLA Modules:
  0.0 169.3 jit_solution(1572744591920512166)
XLA Ops:
  0.6 0.7 reduce_sum.27
  1.3 0.8 copy.37
  2.1 0.1 reduce-precision_convert_fusion.2
  2.2 0.7 convert_element_type.59
  2.9 0.1 copy.39
  3.0 0.1 fusion.19
  3.1 1.8 %pad_maximum_fusion.1.x_ref = bf16[2,32,3712]{2,1,0:T(8,128)(2,1)} fusion(bf16[2,32,128]{2,1,0:T(8,128)(2,1)S(1)} %fusion.19, bf16[2,32,3584]{2,1,0:T(8,128)(2,1)} %param.6), kind=kLoop, calls=%fused_computation.16 | loop fusion | flops 950272 | bytes 950272 | tf_op jit(solution)/shard_map/concatenate | solution.py:483
  4.9 75.0 %shard_map.77 = (bf16[8,4,2,32,3712]{4,3,2,1,0:T(8,128)(2,1)}, bf16[8,72,3584]{2,1,0:T(8,128)(2,1)}, bf16[8,4,2,32,128]{4,3,2,1,0:T(8,128)(2,1)}) custom-call(bf16[2,32,3712]{2,1,0:T(8,128)(2,1)} %pad_maximum_fusion.1.x_ref), custom_call_target="tpu_custom_call" | custom-call | tf_op jit(solution)/shard_map/pallas_call | solution.py:274
  79.9 8.9 %fusion.2 = f32[576,1024]{1,0:T(8,128)S(1)} fusion(bf16[576,3584]{1,0:T(8,128)(2,1)} %bitcast.49, bf16[1,3584,1024]{2,1,0:T(8,128)(2,1)} %param.9), kind=kOutput, calls=%fused_computation.2 | convolution fusion | flops 4227858432 | bytes 13828096 | tf_op jit(solution)/shard_map/dot_general | solution.py:499
  88.9 8.9 %multiply_convert_fusion.hid_ref = bf16[576,1024]{1,0:T(8,128)(2,1)} fusion(f32[576,1024]{1,0:T(8,128)S(1)} %fusion.2, bf16[576,3584]{1,0:T(8,128)(2,1)S(1)} %bitcast.50, bf16[1,3584,1024]{2,1,0:T(8,128)(2,1)} %param.10), kind=kOutput, calls=%fused_computation.4 | convolution fusion | flops 4231397376 | bytes 15007744 | tf_op jit(solution)/shard_map/dot_general | solution.py:500
  97.8 0.1 convert_element_type.64
  97.9 1.5 select_reduce_fusion
  99.6 0.2 fusion.10
  99.8 0.2 compare_reduce_fusion
  100.0 0.1 convolution_convert_fusion
  100.2 0.2 mul.58
  100.3 0.7 mul.59
  101.1 0.1 mul.61
  101.3 0.3 copy.46
  101.6 0.2 reduce-precision_convert_fusion
  101.9 1.2 pad_maximum_fusion.matrix_ref
  103.1 61.8 %shard_map.78 = bf16[7,64,512]{2,1,0:T(8,128)(2,1)} custom-call(bf16[576,1024]{1,0:T(8,128)(2,1)} %multiply_convert_fusion.hid_ref, bf16[1024,3584]{1,0:T(8,128)(2,1)} %bitcast.41, bf16[8,2,256,72]{3,2,1,0:T(8,128)(2,1)} %pad_maximum_fusion.matrix_ref), custom_call_target="tpu_custom_call" | custom-call | tf_op jit(solution)/shard_map/pallas_call | solution.py:431
  164.9 1.3 copy.48
  166.2 1.3 reshape.75
  (16 shorter events, 0.4 us)
Async XLA Ops:
  79.9 9.0 %copy-start.1 = (bf16[8,72,3584]{2,1,0:T(8,128)(2,1)S(1)}, bf16[8,72,3584]{2,1,0:T(8,128)(2,1)}, u32[]{:S(2)}) copy-start(bf16[8,72,3584]{2,1,0:T(8,128)(2,1)} %get-tuple-element.4) | copy-start | bytes 12386308
  88.9 8.9 %copy-start = (bf16[8,4,2,32,128]{4,3,2,1,0:T(8,128)(2,1)S(1)}, bf16[8,4,2,32,128]{4,3,2,1,0:T(8,128)(2,1)}, u32[]{:S(2)}) copy-start(bf16[8,4,2,32,128]{4,3,2,1,0:T(8,128)(2,1)} %get-tuple-element.5) | copy-start | bytes 1572868
where the time goes:
time: 170 us; the launch traced here: 169 us
  Pallas kernels  137 us (81%)
  matrix products  18 us (11%)
  other arithmetic  6.94 us (4%)
  local copies, waits for them, and re-layouts  5.05 us (3%)
  between operations  2.59 us (2%)
    pallas_call x1, Pallas kernels, gather_all(): pl.pallas_call(functools.partial(gather_kernel, planes, capacity, chosen)...  75 us
    pallas_call x1, Pallas kernels, return_all(): pl.pallas_call(functools.partial(return_kernel, planes), out_shape=jax.Sh...  61.8 us
    dot_general x1, matrix products, shards(): gate = jnp.dot(rows, w_gate[0], preferred_element_type=jnp.float32)  8.94 us
    dot_general x1, matrix products, shards(): upper = jnp.dot(rows, w_up[0], preferred_element_type=jnp.float32)  8.89 us

commit v1 on v0

v1 whole, which is shorter than its diff:
```python
import functools

import jax
import jax.numpy as jnp
from jax import lax
from jax.experimental import pallas as pl
from jax.experimental.pallas import tpu as pltpu
from jax.sharding import PartitionSpec as P

route_scale = 2.5
PLANE = 8
SLOTS = 3
LAG = 2
MESH = pl.DeviceIdType.MESH


def tri(size, block):
    row = lax.broadcasted_iota(jnp.int32, (size, size), 0)
    col = lax.broadcasted_iota(jnp.int32, (size, size), 1)
    earlier = (row < col) & (lax.div(row, block) == lax.div(col, block))
    return jnp.where(earlier, 1.0, 0.0).astype(jnp.bfloat16)


def layer_kernel(
    planes,
    capacity,
    tok_mb,
    load_scale,
    x_ref,
    ids_ref,
    scores_ref,
    gate_ref,
    up_ref,
    down_ref,
    out_ref,
    load_ref,
    notes,
    column,
    picks,
    shares,
    packed,
    rows,
    loads,
    loads_in,
    w_gate,
    w_up,
    w_down,
    acc_gate,
    acc_up,
    hid,
    inbox,
    sums_in,
    gate_sem,
    up_sem,
    down_sem,
    n_send,
    n_recv,
    x_send,
    x_recv,
    l_send,
    l_recv,
    d_send,
    d_recv,
    a_send,
    a_recv,
    s_send,
    s_recv,
):
    me = lax.axis_index("ep")
    p = me // PLANE
    q = me % PLANE
    chunks, _, tokens, width = column.shape
    chosen = ids_ref.shape[1]
    spots = packed.shape[2]
    depth = planes * tokens

    def cut(c):
        return pl.ds(pl.multiple_of(c * width, width), width)

    def load_in(c):
        slot = c % SLOTS
        return (
            pltpu.make_async_copy(gate_ref.at[cut(c), :], w_gate.at[slot], gate_sem.at[slot]),
            pltpu.make_async_copy(up_ref.at[cut(c), :], w_up.at[slot], up_sem.at[slot]),
        )

    def load_down(c):
        return pltpu.make_async_copy(down_ref.at[:, cut(c)], w_down.at[c], down_sem.at[c])

    for c in range(SLOTS):
        for copy in load_in(c):
            copy.start()

    barrier = pltpu.get_barrier_semaphore()
    for i in range(1, PLANE):
        other = p * PLANE + (q + i) % PLANE
        pl.semaphore_signal(barrier, inc=1, device_id=(other,), device_id_type=MESH)
    for i in range(1, planes):
        other = ((p + i) % planes) * PLANE + q
        pl.semaphore_signal(barrier, inc=1, device_id=(other,), device_id_type=MESH)

    notes[p] = jnp.zeros(notes.shape[1:], jnp.float32)
    scores = scores_ref[...]
    notes[p, 0, :, :chosen] = ids_ref[...].astype(jnp.float32)
    notes[p, 1, :, :chosen] = route_scale * scores / jnp.sum(scores, axis=1, keepdims=True)

    pl.semaphore_wait(barrier, PLANE + planes - 2)

    def along(i):
        return (p + i) % planes

    def beside(i):
        return (q + i) % PLANE

    def up_down(src, dst, send, recv, i):
        return pltpu.make_async_remote_copy(
            src_ref=src,
            dst_ref=dst,
            send_sem=send,
            recv_sem=recv,
            device_id=(along(i) * PLANE + q,),
            device_id_type=MESH,
        )

    def across(src, dst, send, recv, i):
        return pltpu.make_async_remote_copy(
            src_ref=src,
            dst_ref=dst,
            send_sem=send,
            recv_sem=recv,
            device_id=(p * PLANE + beside(i),),
            device_id_type=MESH,
        )

    def notes_copy(i, at):
        return up_down(notes.at[p], notes.at[at], n_send.at[i], n_recv.at[at], i)

    def x_copy(c, i, at):
        return up_down(x_ref.at[:, cut(c)], column.at[c, at], x_send.at[c, i], x_recv.at[c, at], i)

    def loads_copy(i, at):
        return across(loads.at[beside(i)], loads_in.at[at], l_send.at[i], l_recv.at[at], i)

    def rows_copy(c, i, at):
        return across(packed.at[c, beside(i)], rows.at[c, at], d_send.at[c, i], d_recv.at[c, at], i)

    def answer_copy(c, i, at):
        return across(packed.at[c, beside(i)], inbox.at[c, at], a_send.at[c, i], a_recv.at[c, at], i)

    def sum_copy(c, i, at):
        return up_down(column.at[c, along(i)], sums_in.at[c, at], s_send.at[c, i], s_recv.at[c, at], i)

    for i in range(1, planes):
        notes_copy(i, p).start()

    def send_x(c, carry):
        for i in range(1, planes):
            x_copy(c, i, p).start()
        column[c, p] = x_ref[:, cut(c)]
        return carry

    lax.fori_loop(0, chunks, send_x, 0)

    for c in range(chunks):
        load_down(c).start()

    for i in range(1, planes):
        notes_copy(i, along(i)).wait_recv()

    ids = notes[:, 0].reshape(depth, 128).T[:chosen]
    weights = notes[:, 1].reshape(depth, 128).T[:chosen]
    expert = (p * PLANE + lax.broadcasted_iota(jnp.int32, (PLANE, depth), 0)).astype(jnp.float32)
    named = jnp.zeros((PLANE, depth), jnp.float32)
    share = jnp.zeros((PLANE, depth), jnp.float32)
    for k in range(chosen):
        same = jnp.broadcast_to(ids[k : k + 1], (PLANE, depth)) == expert
        named += jnp.where(same, 1.0, 0.0)
        share += jnp.where(same, jnp.broadcast_to(weights[k : k + 1], (PLANE, depth)), 0.0)
    for j in range(PLANE):
        own = jnp.sum(share[j : j + 1], axis=1, keepdims=True)
        loads[j] = jnp.broadcast_to(own, loads.shape[1:])
    for i in range(1, PLANE):
        loads_copy(i, q).start()

    earlier = tri(128, tok_mb)
    rank = jnp.concatenate(
        [
            jnp.dot(
                named[:, at : at + 128].astype(jnp.bfloat16),
                earlier,
                preferred_element_type=jnp.float32,
            )
            for at in range(0, depth, 128)
        ],
        axis=1,
    )
    start = lax.div(lax.broadcasted_iota(jnp.int32, (PLANE, depth), 1), tok_mb) * capacity
    spot = jnp.where(named > 0.5, start.astype(jnp.float32) + rank, -1.0)
    place = lax.broadcasted_iota(jnp.int32, (spots, depth), 0).astype(jnp.float32)
    for j in range(PLANE):
        found = place == jnp.broadcast_to(spot[j : j + 1], (spots, depth))
        picks[j] = jnp.where(found, 1.0, 0.0).astype(jnp.bfloat16)

    def dispatch(c):
        for i in range(1, planes):
            x_copy(c, i, along(i)).wait_recv()
        tokens_here = column[c].reshape(depth, width)
        found = jnp.dot(
            picks[...].reshape(PLANE * spots, depth),
            tokens_here,
            preferred_element_type=jnp.float32,
        )
        packed[c] = found.reshape(packed.shape[1:]).astype(jnp.bfloat16)
        for i in range(1, PLANE):
            rows_copy(c, i, q).start()
        rows[c, q] = packed[c, q]

    def consume(c):
        for copy in load_in(c):
            copy.wait()
        for i in range(1, PLANE):
            rows_copy(c, i, beside(i)).wait_recv()
        slot = c % SLOTS
        got = rows[c].reshape(PLANE * spots, width)
        acc_gate[...] += jnp.dot(got, w_gate[slot], preferred_element_type=jnp.float32)
        acc_up[...] += jnp.dot(got, w_up[slot], preferred_element_type=jnp.float32)

        @pl.when(c + SLOTS < chunks)
        def _():
            for copy in load_in(c + SLOTS):
                copy.start()

    acc_gate[...] = jnp.zeros(acc_gate.shape, jnp.float32)
    acc_up[...] = jnp.zeros(acc_up.shape, jnp.float32)

    def step(c, carry):
        pl.when(c < chunks)(lambda: dispatch(c))
        pl.when(c >= LAG)(lambda: consume(c - LAG))
        return carry

    lax.fori_loop(0, LAG, step, 0)

    both = jnp.concatenate(
        [spot, share, jnp.zeros((128 - 2 * PLANE, depth), jnp.float32)], axis=0
    ).T
    lane = lax.broadcasted_iota(jnp.int32, (depth, 128), 1).astype(jnp.float32)
    for j in range(PLANE):
        found = lane == jnp.broadcast_to(both[:, j : j + 1], (depth, 128))
        held = jnp.broadcast_to(both[:, PLANE + j : PLANE + j + 1], (depth, 128))
        held = jnp.where(found, held, 0.0)
        high = held.astype(jnp.bfloat16)
        shares[j, 0] = high[:, :spots]
        shares[j, 1] = (held - high.astype(jnp.float32)).astype(jnp.bfloat16)[:, :spots]

    lax.fori_loop(LAG, chunks + LAG, step, 0)

    gate = acc_gate[...]
    hid[...] = (gate / (1.0 + jnp.exp(-gate)) * acc_up[...]).astype(jnp.bfloat16)

    def compute(c, carry):
        load_down(c).wait()
        for i in range(1, PLANE):
            rows_copy(c, i, q).wait_send()
        found = jnp.dot(hid[...], w_down[c], preferred_element_type=jnp.float32)
        packed[c] = found.reshape(packed.shape[1:]).astype(jnp.bfloat16)
        for i in range(1, PLANE):
            answer_copy(c, i, q).start()
        inbox[c, q] = packed[c, q]
        return carry

    lax.fori_loop(0, chunks, compute, 0)

    for i in range(1, PLANE):
        loads_copy(i, beside(i)).wait_recv()
    loads_in[q] = loads[q]
    load_ref[...] = (jnp.sum(loads_in[...], axis=0) * load_scale)[:1, :1]

    def combine(c, carry):
        for i in range(1, PLANE):
            answer_copy(c, i, beside(i)).wait_recv()
        total = jnp.zeros((depth, width), jnp.float32)
        for k in range(PLANE):
            for half in range(2):
                total += jnp.dot(shares[k, half], inbox[c, k], preferred_element_type=jnp.float32)
        column[c] = total.reshape(column.shape[1:]).astype(jnp.bfloat16)
        for i in range(1, planes):
            sum_copy(c, i, p).start()
        sums_in[c, p] = column[c, p]
        return carry

    lax.fori_loop(0, chunks, combine, 0)

    def gather_sums(c, carry):
        for i in range(1, planes):
            sum_copy(c, i, along(i)).wait_recv()
        total = sums_in[c, 0].astype(jnp.float32)
        for k in range(1, planes):
            total += sums_in[c, k].astype(jnp.float32)
        out_ref[:, cut(c)] = total.astype(jnp.bfloat16)
        return carry

    lax.fori_loop(0, chunks, gather_sums, 0)

    for i in range(1, planes):
        notes_copy(i, p).wait_send()
    for i in range(1, PLANE):
        loads_copy(i, q).wait_send()

    def finish(c, carry):
        for i in range(1, PLANE):
            answer_copy(c, i, q).wait_send()
        for i in range(1, planes):
            x_copy(c, i, p).wait_send()
            sum_copy(c, i, p).wait_send()
        return carry

    lax.fori_loop(0, chunks, finish, 0)


def layer(x, ids, scores, gate, up, down, devices, tok_mb, capacity, load_scale):
    planes = devices // PLANE
    tokens, model_width = x.shape
    inner = gate.shape[1]
    width = next(w for w in (512, 256, 128) if model_width % w == 0)
    chunks = model_width // width
    spots = planes * (tokens // tok_mb) * capacity
    dma = pltpu.SemaphoreType.DMA
    vmem = pl.BlockSpec(memory_space=pltpu.VMEM)
    hbm = pl.BlockSpec(memory_space=pl.ANY)
    bf16, f32 = jnp.bfloat16, jnp.float32
    return pl.pallas_call(
        functools.partial(layer_kernel, planes, capacity, tok_mb, load_scale),
        out_shape=(
            jax.ShapeDtypeStruct((tokens, model_width), bf16),
            jax.ShapeDtypeStruct((1, 1), f32),
        ),
        in_specs=[vmem, vmem, vmem, hbm, hbm, hbm],
        out_specs=(vmem, vmem),
        scratch_shapes=[
            pltpu.VMEM((planes, 2, tokens, 128), f32),
            pltpu.VMEM((chunks, planes, tokens, width), bf16),
            pltpu.VMEM((PLANE, spots, planes * tokens), bf16),
            pltpu.VMEM((PLANE, 2, planes * tokens, spots), bf16),
            pltpu.VMEM((chunks, PLANE, spots, width), bf16),
            pltpu.VMEM((chunks, PLANE, spots, width), bf16),
            pltpu.VMEM((PLANE, 8, 128), f32),
            pltpu.VMEM((PLANE, 8, 128), f32),
            pltpu.VMEM((SLOTS, width, inner), bf16),
            pltpu.VMEM((SLOTS, width, inner), bf16),
            pltpu.VMEM((chunks, inner, width), bf16),
            pltpu.VMEM((PLANE * spots, inner), f32),
            pltpu.VMEM((PLANE * spots, inner), f32),
            pltpu.VMEM((PLANE * spots, inner), bf16),
            pltpu.VMEM((chunks, PLANE, spots, width), bf16),
            pltpu.VMEM((chunks, planes, tokens, width), bf16),
            dma((SLOTS,)),
            dma((SLOTS,)),
            dma((chunks,)),
            dma((planes,)),
            dma((planes,)),
            dma((chunks, planes)),
            dma((chunks, planes)),
            dma((PLANE,)),
            dma((PLANE,)),
            dma((chunks, PLANE)),
            dma((chunks, PLANE)),
            dma((chunks, PLANE)),
            dma((chunks, PLANE)),
            dma((chunks, planes)),
            dma((chunks, planes)),
        ],
        compiler_params=pltpu.CompilerParams(
            collective_id=0, has_side_effects=True, vmem_limit_bytes=66 * 1000 * 1000
        ),
    )(x, ids, scores, gate, up, down)


def shards(hidden, expert_ids, gate_scores, w_gate, w_up, w_down):
    devices = lax.axis_size("ep")
    micro_count, tok_mb, model_width = hidden.shape
    chosen = expert_ids.shape[2]
    capacity = tok_mb * chosen // devices + 1
    tokens = micro_count * tok_mb
    mixed, expert_load = layer(
        hidden.reshape(tokens, model_width),
        expert_ids.reshape(tokens, chosen),
        gate_scores.reshape(tokens, chosen),
        w_gate[0],
        w_up[0],
        w_down[0],
        devices,
        tok_mb,
        capacity,
        devices / (route_scale * tokens * devices),
    )
    return (mixed.reshape(micro_count, tok_mb, model_width), expert_load.reshape(1))


def solution(mesh):
    placed = (
        P(None, "ep", None),
        P(None, "ep", None),
        P(None, "ep", None),
        P("ep", None, None),
        P("ep", None, None),
        P("ep", None, None),
    )
    return jax.shard_map(
        shards,
        mesh=mesh,
        in_specs=placed,
        out_specs=(P(None, "ep", None), P("ep")),
        check_vma=False,
    )
```

time: 170 us -> 140 us (0.82)
  matrix products: 18 us -> 0 us
  other arithmetic: 6.94 us -> 0 us
  Pallas kernels: 137 us -> 132 us
    dot_general x3 -> x0, matrix products: 18 us -> none  [the longest x1 8.94 us: shards(): gate = jnp.dot(rows, w_gate[0], preferred_element_type=jnp.float32)]
    pallas_call x2 -> x1, Pallas kernels: 137 us -> 132 us  [layer(): pl.pallas_call(functools.partial(layer_kernel, planes, capacity, tok_mb,...]
    unnamed x5 -> x3, local copies, waits for them, and re-layouts: 0.78 us -> 4.59 us
    reduce_sum x3 -> x0, other arithmetic: 2.37 us -> none  [the longest x1 1.48 us: shards(): jnp.sum(jnp.where(named, all_weights, 0.0)).reshape(1)]
    concatenate x2 -> x0, other arithmetic: 1.92 us -> none  [the longest x1 1.83 us: shards(): jnp.concatenate([hidden, extra], axis=-1)]
where the time goes in v1:
time: 140 us; the launch traced here: 139 us
  Pallas kernels  132 us (94%)
  local copies, waits for them, and re-layouts  4.59 us (3%)
  between operations  2.38 us (2%)
    pallas_call x1, Pallas kernels, layer(): pl.pallas_call(functools.partial(layer_kernel, planes, capacity, tok_mb,...  132 us
    unnamed x3, local copies, waits for them, and re-layouts  4.59 us

profile of v1, /device:TPU:0, one launch (start us, length us, event | category | flops | bytes accessed | tf_op | source)
XLA Modules:
  0.0 138.8 jit_solution(8919085574928088492)
XLA Ops:
  0.6 1.4 %copy.8 = s32[2,32,8]{2,1,0:T(8,128)} copy(s32[2,32,8]{1,2,0:T(8,128)} %param.7) | data formatting | bytes 4096 | tf_op args[1]
  2.0 1.4 copy.9
  3.4 131.8 %shard_map.77 = (bf16[64,3584]{1,0:T(8,128)(2,1)}, f32[1,1]{1,0:T(1,128)}) custom-call(bf16[64,3584]{1,0:T(8,128)(2,1)} %bitcast.12, s32[64,8]{1,0:T(8,128)} %bitcast.13, f32[64,8]{1,0:T(8,128)} %bitcast.14, bf16[3584,1024]{1,0:T(8,128)(2,1)} %bitcast.8, bf16[3584,1024]{1,0:T(8,128)(2,1)} %bitcast.9, bf16[1024,3584]{1,0:T(8,128)(2,1)} %bitcast.10), custom_call_target="tpu_custom_call" | custom-call | tf_op jit(solution)/shard_map/pallas_call | solution.py:331
  135.2 1.8 %copy.12 = bf16[2,32,3584]{2,1,0:T(8,128)(2,1)} copy(bf16[2,32,3584]{2,1,0:T(8,128)(2,1)} %bitcast.11) | data formatting | bytes 917504

commit v2 on v1

--- a/solution.py
+++ b/solution.py
@@ -10,7 +10,7 @@
 route_scale = 2.5
 PLANE = 8
 SLOTS = 3
-LAG = 2
+LAG = 3
 MESH = pl.DeviceIdType.MESH
 
 
@@ -26,7 +26,7 @@
     capacity,
     tok_mb,
     load_scale,
-    x_ref,
+    hidden_ref,
     ids_ref,
     scores_ref,
     gate_ref,
@@ -34,6 +34,7 @@
     down_ref,
     out_ref,
     load_ref,
+    x_ref,
     notes,
     column,
     picks,
@@ -50,6 +51,7 @@
     hid,
     inbox,
     sums_in,
+    hidden_sem,
     gate_sem,
     up_sem,
     down_sem,
@@ -70,7 +72,7 @@
     p = me // PLANE
     q = me % PLANE
     chunks, _, tokens, width = column.shape
-    chosen = ids_ref.shape[1]
+    micro_count, chosen, _ = ids_ref.shape
     spots = packed.shape[2]
     depth = planes * tokens
 
@@ -87,9 +89,8 @@
     def load_down(c):
         return pltpu.make_async_copy(down_ref.at[:, cut(c)], w_down.at[c], down_sem.at[c])
 
-    for c in range(SLOTS):
-        for copy in load_in(c):
-            copy.start()
+    hidden_copy = pltpu.make_async_copy(hidden_ref, x_ref, hidden_sem)
+    hidden_copy.start()
 
     barrier = pltpu.get_barrier_semaphore()
     for i in range(1, PLANE):
@@ -99,10 +100,16 @@
         other = ((p + i) % planes) * PLANE + q
         pl.semaphore_signal(barrier, inc=1, device_id=(other,), device_id_type=MESH)
 
+    for c in range(SLOTS):
+        for copy in load_in(c):
+            copy.start()
+
     notes[p] = jnp.zeros(notes.shape[1:], jnp.float32)
-    scores = scores_ref[...]
-    notes[p, 0, :, :chosen] = ids_ref[...].astype(jnp.float32)
-    notes[p, 1, :, :chosen] = route_scale * scores / jnp.sum(scores, axis=1, keepdims=True)
+    for m in range(micro_count):
+        scores = scores_ref[m]
+        notes[p, m, 0, :, :tok_mb] = ids_ref[m].astype(jnp.float32)
+        notes[p, m, 1, :, :tok_mb] = route_scale * scores / jnp.sum(scores, axis=0, keepdims=True)
+    hidden_copy.wait()
 
     pl.semaphore_wait(barrier, PLANE + planes - 2)
 
@@ -167,8 +174,17 @@
     for i in range(1, planes):
         notes_copy(i, along(i)).wait_recv()
 
-    ids = notes[:, 0].reshape(depth, 128).T[:chosen]
-    weights = notes[:, 1].reshape(depth, 128).T[:chosen]
+    def spread(part):
+        pieces = [notes[at, m, part] for at in range(planes) for m in range(micro_count)]
+        lanes = []
+        for at in range(0, len(pieces), 128 // tok_mb):
+            block = pieces[at]
+            for k, piece in enumerate(pieces[at + 1 : at + 128 // tok_mb]):
+                block += pltpu.roll(piece, (k + 1) * tok_mb, 1)
+            lanes.append(block)
+        return jnp.concatenate(lanes, axis=1)
+
+    ids, weights = spread(0), spread(1)
     expert = (p * PLANE + lax.broadcasted_iota(jnp.int32, (PLANE, depth), 0)).astype(jnp.float32)
     named = jnp.zeros((PLANE, depth), jnp.float32)
     share = jnp.zeros((PLANE, depth), jnp.float32)
@@ -321,7 +337,7 @@
     planes = devices // PLANE
     tokens, model_width = x.shape
     inner = gate.shape[1]
-    width = next(w for w in (512, 256, 128) if model_width % w == 0)
+    width = next(w for w in (256, 128) if model_width % w == 0)
     chunks = model_width // width
     spots = planes * (tokens // tok_mb) * capacity
     dma = pltpu.SemaphoreType.DMA
@@ -334,10 +350,11 @@
             jax.ShapeDtypeStruct((tokens, model_width), bf16),
             jax.ShapeDtypeStruct((1, 1), f32),
         ),
-        in_specs=[vmem, vmem, vmem, hbm, hbm, hbm],
+        in_specs=[hbm, vmem, vmem, hbm, hbm, hbm],
         out_specs=(vmem, vmem),
         scratch_shapes=[
-            pltpu.VMEM((planes, 2, tokens, 128), f32),
+            pltpu.VMEM((tokens, model_width), bf16),
+            pltpu.VMEM((planes, tokens // tok_mb, 2, ids.shape[1], 128), f32),
             pltpu.VMEM((chunks, planes, tokens, width), bf16),
             pltpu.VMEM((PLANE, spots, planes * tokens), bf16),
             pltpu.VMEM((PLANE, 2, planes * tokens, spots), bf16),
@@ -353,6 +370,7 @@
             pltpu.VMEM((PLANE * spots, inner), bf16),
             pltpu.VMEM((chunks, PLANE, spots, width), bf16),
             pltpu.VMEM((chunks, planes, tokens, width), bf16),
+            dma,
             dma((SLOTS,)),
             dma((SLOTS,)),
             dma((chunks,)),
@@ -383,8 +401,8 @@
     tokens = micro_count * tok_mb
     mixed, expert_load = layer(
         hidden.reshape(tokens, model_width),
-        expert_ids.reshape(tokens, chosen),
-        gate_scores.reshape(tokens, chosen),
+        expert_ids.transpose(0, 2, 1),
+        gate_scores.transpose(0, 2, 1),
         w_gate[0],
         w_up[0],
         w_down[0],

time: 140 us -> 129 us (0.921)
  Pallas kernels: 132 us -> 125 us
  local copies, waits for them, and re-layouts: 4.59 us -> 1.82 us
    pallas_call x1, Pallas kernels: 132 us -> 125 us  [layer(): pl.pallas_call(functools.partial(layer_kernel, planes, capacity, tok_mb,...]
    unnamed x3 -> x1, local copies, waits for them, and re-layouts: 4.59 us -> 1.82 us
where the time goes in v2:
time: 129 us
  Pallas kernels  125 us (97%)
  between operations  2.46 us (2%)
  local copies, waits for them, and re-layouts  1.82 us (1%)
    pallas_call x1, Pallas kernels, layer(): pl.pallas_call(functools.partial(layer_kernel, planes, capacity, tok_mb,...  125 us

profile of v2, /device:TPU:0, one launch (start us, length us, event | category | flops | bytes accessed | tf_op | source)
XLA Modules:
  0.0 129.1 jit_solution(16588978868668426119)
XLA Ops:
  0.6 124.8 %shard_map.77 = (bf16[64,3584]{1,0:T(8,128)(2,1)}, f32[1,1]{1,0:T(1,128)}) custom-call(bf16[64,3584]{1,0:T(8,128)(2,1)} %bitcast.12, s32[2,8,32]{2,1,0:T(8,128)} %bitcast.13, f32[2,8,32]{2,1,0:T(8,128)} %bitcast.14, bf16[3584,1024]{1,0:T(8,128)(2,1)} %bitcast.8, bf16[3584,1024]{1,0:T(8,128)(2,1)} %bitcast.9, bf16[1024,3584]{1,0:T(8,128)(2,1)} %bitcast.10), custom_call_target="tpu_custom_call" | custom-call | tf_op jit(solution)/shard_map/pallas_call | solution.py:347
  125.5 1.8 %copy.10 = bf16[2,32,3584]{2,1,0:T(8,128)(2,1)} copy(bf16[2,32,3584]{2,1,0:T(8,128)(2,1)} %bitcast.11) | data formatting | bytes 917504

commit v3 on v2

--- a/solution.py
+++ b/solution.py
@@ -86,8 +86,7 @@
             pltpu.make_async_copy(up_ref.at[cut(c), :], w_up.at[slot], up_sem.at[slot]),
         )
 
-    def load_down(c):
-        return pltpu.make_async_copy(down_ref.at[:, cut(c)], w_down.at[c], down_sem.at[c])
+    load_down = pltpu.make_async_copy(down_ref, w_down, down_sem)
 
     hidden_copy = pltpu.make_async_copy(hidden_ref, x_ref, hidden_sem)
     hidden_copy.start()
@@ -139,40 +138,43 @@
             device_id_type=MESH,
         )
 
-    def notes_copy(i, at):
-        return up_down(notes.at[p], notes.at[at], n_send.at[i], n_recv.at[at], i)
-
-    def x_copy(c, i, at):
-        return up_down(x_ref.at[:, cut(c)], column.at[c, at], x_send.at[c, i], x_recv.at[c, at], i)
-
-    def loads_copy(i, at):
-        return across(loads.at[beside(i)], loads_in.at[at], l_send.at[i], l_recv.at[at], i)
-
-    def rows_copy(c, i, at):
-        return across(packed.at[c, beside(i)], rows.at[c, at], d_send.at[c, i], d_recv.at[c, at], i)
-
-    def answer_copy(c, i, at):
-        return across(packed.at[c, beside(i)], inbox.at[c, at], a_send.at[c, i], a_recv.at[c, at], i)
-
-    def sum_copy(c, i, at):
-        return up_down(column.at[c, along(i)], sums_in.at[c, at], s_send.at[c, i], s_recv.at[c, at], i)
+    def notes_copy(i):
+        return up_down(notes.at[p], notes.at[p], n_send, n_recv, i)
+
+    def x_copy(c, i):
+        return up_down(x_ref.at[:, cut(c)], column.at[c, p], x_send, x_recv.at[c], i)
+
+    def loads_copy(i):
+        return across(loads.at[beside(i)], loads_in.at[q], l_send, l_recv, i)
+
+    def rows_copy(c, i):
+        return across(packed.at[c, beside(i)], rows.at[c, q], d_send.at[c], d_recv.at[c], i)
+
+    def answer_copy(c, i):
+        return across(packed.at[c, beside(i)], inbox.at[c, q], a_send, a_recv.at[c], i)
+
+    def sum_copy(c, i):
+        return up_down(column.at[c, along(i)], sums_in.at[c, p], s_send, s_recv.at[c], i)
+
+    def arrived(ref, sem):
+        across(ref, ref, sem, sem, 1).wait_recv()
+
+    def sent(ref, sem):
+        across(ref, ref, sem, sem, 1).wait_send()
 
     for i in range(1, planes):
-        notes_copy(i, p).start()
+        notes_copy(i).start()
 
     def send_x(c, carry):
         for i in range(1, planes):
-            x_copy(c, i, p).start()
+            x_copy(c, i).start()
         column[c, p] = x_ref[:, cut(c)]
         return carry
 
     lax.fori_loop(0, chunks, send_x, 0)
 
-    for c in range(chunks):
-        load_down(c).start()
-
-    for i in range(1, planes):
-        notes_copy(i, along(i)).wait_recv()
+    load_down.start()
+    arrived(notes.at[pl.ds(0, planes - 1)], n_recv)
 
     def spread(part):
         pieces = [notes[at, m, part] for at in range(planes) for m in range(micro_count)]
@@ -196,7 +198,7 @@
         own = jnp.sum(share[j : j + 1], axis=1, keepdims=True)
         loads[j] = jnp.broadcast_to(own, loads.shape[1:])
     for i in range(1, PLANE):
-        loads_copy(i, q).start()
+        loads_copy(i).start()
 
     earlier = tri(128, tok_mb)
     rank = jnp.concatenate(
@@ -218,8 +220,7 @@
         picks[j] = jnp.where(found, 1.0, 0.0).astype(jnp.bfloat16)
 
     def dispatch(c):
-        for i in range(1, planes):
-            x_copy(c, i, along(i)).wait_recv()
+        arrived(column.at[c, pl.ds(0, planes - 1)], x_recv.at[c])
         tokens_here = column[c].reshape(depth, width)
         found = jnp.dot(
             picks[...].reshape(PLANE * spots, depth),
@@ -228,14 +229,13 @@
         )
         packed[c] = found.reshape(packed.shape[1:]).astype(jnp.bfloat16)
         for i in range(1, PLANE):
-            rows_copy(c, i, q).start()
+            rows_copy(c, i).start()
         rows[c, q] = packed[c, q]
 
     def consume(c):
         for copy in load_in(c):
             copy.wait()
-        for i in range(1, PLANE):
-            rows_copy(c, i, beside(i)).wait_recv()
+        arrived(rows.at[c, pl.ds(0, PLANE - 1)], d_recv.at[c])
         slot = c % SLOTS
         got = rows[c].reshape(PLANE * spots, width)
         acc_gate[...] += jnp.dot(got, w_gate[slot], preferred_element_type=jnp.float32)
@@ -273,42 +273,39 @@
     gate = acc_gate[...]
     hid[...] = (gate / (1.0 + jnp.exp(-gate)) * acc_up[...]).astype(jnp.bfloat16)
 
+    load_down.wait()
+
     def compute(c, carry):
-        load_down(c).wait()
-        for i in range(1, PLANE):
-            rows_copy(c, i, q).wait_send()
-        found = jnp.dot(hid[...], w_down[c], preferred_element_type=jnp.float32)
+        sent(packed.at[c, pl.ds(0, PLANE - 1)], d_send.at[c])
+        found = jnp.dot(hid[...], w_down[:, cut(c)], preferred_element_type=jnp.float32)
         packed[c] = found.reshape(packed.shape[1:]).astype(jnp.bfloat16)
         for i in range(1, PLANE):
-            answer_copy(c, i, q).start()
+            answer_copy(c, i).start()
         inbox[c, q] = packed[c, q]
         return carry
 
     lax.fori_loop(0, chunks, compute, 0)
 
-    for i in range(1, PLANE):
-        loads_copy(i, beside(i)).wait_recv()
+    arrived(loads_in.at[pl.ds(0, PLANE - 1)], l_recv)
     loads_in[q] = loads[q]
     load_ref[...] = (jnp.sum(loads_in[...], axis=0) * load_scale)[:1, :1]
 
     def combine(c, carry):
-        for i in range(1, PLANE):
-            answer_copy(c, i, beside(i)).wait_recv()
+        arrived(inbox.at[c, pl.ds(0, PLANE - 1)], a_recv.at[c])
         total = jnp.zeros((depth, width), jnp.float32)
         for k in range(PLANE):
             for half in range(2):
                 total += jnp.dot(shares[k, half], inbox[c, k], preferred_element_type=jnp.float32)
         column[c] = total.reshape(column.shape[1:]).astype(jnp.bfloat16)
         for i in range(1, planes):
-            sum_copy(c, i, p).start()
+            sum_copy(c, i).start()
         sums_in[c, p] = column[c, p]
         return carry
 
     lax.fori_loop(0, chunks, combine, 0)
 
     def gather_sums(c, carry):
-        for i in range(1, planes):
-            sum_copy(c, i, along(i)).wait_recv()
+        arrived(sums_in.at[c, pl.ds(0, planes - 1)], s_recv.at[c])
         total = sums_in[c, 0].astype(jnp.float32)
         for k in range(1, planes):
             total += sums_in[c, k].astype(jnp.float32)
@@ -317,20 +314,11 @@
 
     lax.fori_loop(0, chunks, gather_sums, 0)
 
-    for i in range(1, planes):
-        notes_copy(i, p).wait_send()
-    for i in range(1, PLANE):
-        loads_copy(i, q).wait_send()
-
-    def finish(c, carry):
-        for i in range(1, PLANE):
-            answer_copy(c, i, q).wait_send()
-        for i in range(1, planes):
-            x_copy(c, i, p).wait_send()
-            sum_copy(c, i, p).wait_send()
-        return carry
-
-    lax.fori_loop(0, chunks, finish, 0)
+    sent(notes.at[pl.ds(0, planes - 1)], n_send)
+    sent(loads.at[pl.ds(0, PLANE - 1)], l_send)
+    sent(column.at[:, pl.ds(0, planes - 1)], x_send)
+    sent(column.at[:, pl.ds(0, planes - 1)], s_send)
+    sent(packed.at[:, pl.ds(0, PLANE - 1)], a_send)
 
 
 def layer(x, ids, scores, gate, up, down, devices, tok_mb, capacity, load_scale):
@@ -364,7 +352,7 @@
             pltpu.VMEM((PLANE, 8, 128), f32),
             pltpu.VMEM((SLOTS, width, inner), bf16),
             pltpu.VMEM((SLOTS, width, inner), bf16),
-            pltpu.VMEM((chunks, inner, width), bf16),
+            pltpu.VMEM((inner, model_width), bf16),
             pltpu.VMEM((PLANE * spots, inner), f32),
             pltpu.VMEM((PLANE * spots, inner), f32),
             pltpu.VMEM((PLANE * spots, inner), bf16),
@@ -373,19 +361,19 @@
             dma,
             dma((SLOTS,)),
             dma((SLOTS,)),
+            dma,
+            dma,
+            dma,
+            dma,
             dma((chunks,)),
-            dma((planes,)),
-            dma((planes,)),
-            dma((chunks, planes)),
-            dma((chunks, planes)),
-            dma((PLANE,)),
-            dma((PLANE,)),
-            dma((chunks, PLANE)),
-            dma((chunks, PLANE)),
-            dma((chunks, PLANE)),
-            dma((chunks, PLANE)),
-            dma((chunks, planes)),
-            dma((chunks, planes)),
+            dma,
+            dma,
+            dma((chunks,)),
+            dma((chunks,)),
+            dma,
+            dma((chunks,)),
+            dma,
+            dma((chunks,)),
         ],
         compiler_params=pltpu.CompilerParams(
             collective_id=0, has_side_effects=True, vmem_limit_bytes=66 * 1000 * 1000

time: 129 us -> 123 us (0.953)
  Pallas kernels: 125 us -> 119 us
    pallas_call x1, Pallas kernels: 125 us -> 119 us  [layer(): pl.pallas_call(functools.partial(layer_kernel, planes, capacity, tok_mb,...]
where the time goes in v3:
time: 123 us
  Pallas kernels  119 us (97%)
  between operations  2.46 us (2%)
  local copies, waits for them, and re-layouts  1.82 us (1%)
    pallas_call x1, Pallas kernels, layer(): pl.pallas_call(functools.partial(layer_kernel, planes, capacity, tok_mb,...  119 us

profile of v3, /device:TPU:0, one launch (start us, length us, event | category | flops | bytes accessed | tf_op | source)
XLA Modules:
  0.0 123.1 jit_solution(16617727072360159209)
XLA Ops:
  0.6 118.8 %shard_map.77 = (bf16[64,3584]{1,0:T(8,128)(2,1)}, f32[1,1]{1,0:T(1,128)}) custom-call(bf16[64,3584]{1,0:T(8,128)(2,1)} %bitcast.12, s32[2,8,32]{2,1,0:T(8,128)} %bitcast.13, f32[2,8,32]{2,1,0:T(8,128)} %bitcast.14, bf16[3584,1024]{1,0:T(8,128)(2,1)} %bitcast.8, bf16[3584,1024]{1,0:T(8,128)(2,1)} %bitcast.9, bf16[1024,3584]{1,0:T(8,128)(2,1)} %bitcast.10), custom_call_target="tpu_custom_call" | custom-call | tf_op jit(solution)/shard_map/pallas_call | solution.py:335
  119.5 1.8 %copy.10 = bf16[2,32,3584]{2,1,0:T(8,128)(2,1)} copy(bf16[2,32,3584]{2,1,0:T(8,128)(2,1)} %bitcast.11) | data formatting | bytes 917504

commit v4 on v3

v4 whole, which is shorter than its diff:
```python
import functools

import jax
import jax.numpy as jnp
from jax import lax
from jax.experimental import pallas as pl
from jax.experimental.pallas import tpu as pltpu
from jax.sharding import PartitionSpec as P

route_scale = 2.5
PLANE = 8
SLOTS = 3
LAG = 3
QUADS = PLANE // 2
FLIPPED = 2
MESH = pl.DeviceIdType.MESH


class Route:
    def __init__(self, gather_at, gather_of, scatter_at, scatter_of, notes, picks, shares):
        self.gather_at, self.gather_of = gather_at, gather_of
        self.scatter_at, self.scatter_of = scatter_at, scatter_of
        self.notes, self.picks, self.shares = notes, picks, shares


def tri(size, block):
    row = lax.broadcasted_iota(jnp.int32, (size, size), 0)
    col = lax.broadcasted_iota(jnp.int32, (size, size), 1)
    earlier = (row < col) & (lax.div(row, block) == lax.div(col, block))
    return jnp.where(earlier, 1.0, 0.0).astype(jnp.bfloat16)


def layer_kernel(
    planes,
    capacity,
    tok_mb,
    load_scale,
    flipped,
    hidden_ref,
    ids_ref,
    scores_ref,
    gate_ref,
    up_ref,
    down_ref,
    out_ref,
    load_ref,
    x_ref,
    notes,
    column,
    picks,
    shares,
    notes_f,
    picks_f,
    shares_f,
    perm,
    packed,
    rows,
    loads,
    loads_in,
    w_gate,
    w_up,
    w_down,
    acc_gate,
    acc_up,
    hid,
    inbox,
    sums_in,
    hidden_sem,
    gate_sem,
    up_sem,
    down_sem,
    n_send,
    n_recv,
    f_send,
    f_recv,
    x_send,
    x_recv,
    l_send,
    l_recv,
    d_send,
    d_recv,
    a_send,
    a_recv,
    s_send,
    s_recv,
):
    me = lax.axis_index("ep")
    p = me // PLANE
    q = me % PLANE
    quad, core = q // 2, q % 2
    chunks, _, tokens, width = column.shape
    micro_count, chosen, _ = ids_ref.shape
    spots = packed.shape[2]
    depth = planes * tokens
    straight = chunks - flipped

    def cut(c):
        return pl.ds(pl.multiple_of(c * width, width), width)

    def load_in(c):
        slot = c % SLOTS
        return (
            pltpu.make_async_copy(gate_ref.at[cut(c), :], w_gate.at[slot], gate_sem.at[slot]),
            pltpu.make_async_copy(up_ref.at[cut(c), :], w_up.at[slot], up_sem.at[slot]),
        )

    load_down = pltpu.make_async_copy(down_ref, w_down, down_sem)

    hidden_copy = pltpu.make_async_copy(hidden_ref, x_ref, hidden_sem)
    hidden_copy.start()

    turn = p * 2 + core
    ahead = Route(
        p,
        lambda i: ((p + i) % planes, ((p + i) % planes) * PLANE + q),
        q,
        lambda i: ((q + i) % PLANE, p * PLANE + (q + i) % PLANE),
        notes,
        picks,
        shares,
    )
    aside = Route(
        quad,
        lambda i: ((quad + i) % QUADS, p * PLANE + ((quad + i) % QUADS) * 2 + core),
        turn,
        lambda i: (
            (turn + i) % (2 * planes),
            ((turn + i) % (2 * planes)) // 2 * PLANE + quad * 2 + (turn + i) % 2,
        ),
        notes_f,
        picks_f,
        shares_f,
    )

    barrier = pltpu.get_barrier_semaphore()

    def greet(other):
        pl.semaphore_signal(barrier, inc=1, device_id=(other,), device_id_type=MESH)

    for i in range(1, PLANE):
        greet(ahead.scatter_of(i)[1])
    for i in range(1, planes):
        greet(ahead.gather_of(i)[1])
    if flipped:
        for i in range(1, planes):
            greet(((p + i) % planes) * PLANE + quad * 2 + 1 - core)

    for c in range(SLOTS):
        for copy in load_in(c):
            copy.start()

    notes[p] = jnp.zeros(notes.shape[1:], jnp.float32)
    for m in range(micro_count):
        scores = scores_ref[m]
        notes[p, m, 0, :, :tok_mb] = ids_ref[m].astype(jnp.float32)
        notes[p, m, 1, :, :tok_mb] = route_scale * scores / jnp.sum(scores, axis=0, keepdims=True)
    if flipped:
        notes_f[quad] = notes[p]
    hidden_copy.wait()

    pl.semaphore_wait(barrier, PLANE + planes - 2 + (planes - 1 if flipped else 0))

    def remote(src, dst, send, recv, other):
        return pltpu.make_async_remote_copy(
            src_ref=src,
            dst_ref=dst,
            send_sem=send,
            recv_sem=recv,
            device_id=(other,),
            device_id_type=MESH,
        )

    def notes_copy(way, i, send, recv):
        mine = way.notes.at[way.gather_at]
        return remote(mine, mine, send, recv, way.gather_of(i)[1])

    def x_copy(way, c, i):
        place = column.at[c, way.gather_at]
        return remote(x_ref.at[:, cut(c)], place, x_send, x_recv.at[c], way.gather_of(i)[1])

    def loads_copy(i):
        at, other = ahead.scatter_of(i)
        return remote(loads.at[at], loads_in.at[q], l_send, l_recv, other)

    def rows_copy(way, c, i):
        at, other = way.scatter_of(i)
        place = rows.at[c, way.scatter_at]
        return remote(packed.at[c, at], place, d_send.at[c], d_recv.at[c], other)

    def answer_copy(way, c, i):
        at, other = way.scatter_of(i)
        place = inbox.at[c, way.scatter_at]
        return remote(packed.at[c, at], place, a_send, a_recv.at[c], other)

    def sum_copy(way, c, i):
        at, other = way.gather_of(i)
        place = sums_in.at[c, way.gather_at]
        return remote(column.at[c, at], place, s_send, s_recv.at[c], other)

    def arrived(ref, sem):
        remote(ref, ref, sem, sem, ahead.scatter_of(1)[1]).wait_recv()

    def sent(ref, sem):
        remote(ref, ref, sem, sem, ahead.scatter_of(1)[1]).wait_send()

    for i in range(1, planes):
        notes_copy(ahead, i, n_send, n_recv).start()

    def send_x(way, c):
        for i in range(1, planes):
            x_copy(way, c, i).start()
        column[c, way.gather_at] = x_ref[:, cut(c)]

    def send_ahead(c, carry):
        send_x(ahead, c)
        return carry

    if flipped:
        for i in range(1, QUADS):
            notes_copy(aside, i, f_send, f_recv).start()
        for c in range(straight, chunks):
            send_x(aside, c)
    lax.fori_loop(0, straight, send_ahead, 0)

    load_down.start()
    arrived(notes.at[pl.ds(0, planes - 1)], n_recv)

    earlier = tri(128, tok_mb)

    def spread(way, part):
        pieces = [way.notes[at, m, part] for at in range(planes) for m in range(micro_count)]
        lanes = []
        for at in range(0, len(pieces), 128 // tok_mb):
            block = pieces[at]
            for k, piece in enumerate(pieces[at + 1 : at + 128 // tok_mb]):
                block += pltpu.roll(piece, (k + 1) * tok_mb, 1)
            lanes.append(block)
        return jnp.concatenate(lanes, axis=1)

    def prepare(way, expert):
        ids, weights = spread(way, 0), spread(way, 1)
        named = jnp.zeros((PLANE, depth), jnp.float32)
        share = jnp.zeros((PLANE, depth), jnp.float32)
        for k in range(chosen):
            same = jnp.broadcast_to(ids[k : k + 1], (PLANE, depth)) == expert
            named += jnp.where(same, 1.0, 0.0)
            share += jnp.where(same, jnp.broadcast_to(weights[k : k + 1], (PLANE, depth)), 0.0)
        rank = jnp.concatenate(
            [
                jnp.dot(
                    named[:, at : at + 128].astype(jnp.bfloat16),
                    earlier,
                    preferred_element_type=jnp.float32,
                )
                for at in range(0, depth, 128)
            ],
            axis=1,
        )
        start = lax.div(lax.broadcasted_iota(jnp.int32, (PLANE, depth), 1), tok_mb) * capacity
        spot = jnp.where(named > 0.5, start.astype(jnp.float32) + rank, -1.0)
        place = lax.broadcasted_iota(jnp.int32, (spots, depth), 0).astype(jnp.float32)
        for j in range(PLANE):
            found = place == jnp.broadcast_to(spot[j : j + 1], (spots, depth))
            way.picks[j] = jnp.where(found, 1.0, 0.0).astype(jnp.bfloat16)
        return spot, share

    def weigh(way, spot, share):
        both = jnp.concatenate(
            [spot, share, jnp.zeros((128 - 2 * PLANE, depth), jnp.float32)], axis=0
        ).T
        lane = lax.broadcasted_iota(jnp.int32, (depth, 128), 1).astype(jnp.float32)
        for j in range(PLANE):
            found = lane == jnp.broadcast_to(both[:, j : j + 1], (depth, 128))
            held = jnp.broadcast_to(both[:, PLANE + j : PLANE + j + 1], (depth, 128))
            held = jnp.where(found, held, 0.0)
            high = held.astype(jnp.bfloat16)
            way.shares[j, 0] = high[:, :spots]
            way.shares[j, 1] = (held - high.astype(jnp.float32)).astype(jnp.bfloat16)[:, :spots]

    index = lax.broadcasted_iota(jnp.int32, (PLANE, depth), 0)
    spot, share = prepare(ahead, (p * PLANE + index).astype(jnp.float32))
    for j in range(PLANE):
        own = jnp.sum(share[j : j + 1], axis=1, keepdims=True)
        loads[j] = jnp.broadcast_to(own, loads.shape[1:])
    for i in range(1, PLANE):
        loads_copy(i).start()

    def dispatch(way, c):
        arrived(column.at[c, pl.ds(0, planes - 1)], x_recv.at[c])
        tokens_here = column[c].reshape(depth, width)
        found = jnp.dot(
            way.picks[...].reshape(PLANE * spots, depth),
            tokens_here,
            preferred_element_type=jnp.float32,
        )
        packed[c] = found.reshape(packed.shape[1:]).astype(jnp.bfloat16)
        for i in range(1, PLANE):
            rows_copy(way, c, i).start()
        rows[c, way.scatter_at] = packed[c, way.scatter_at]

    def reorder(values):
        return jnp.dot(perm[...], values, preferred_element_type=jnp.float32).astype(jnp.bfloat16)

    def consume(way, c):
        for copy in load_in(c):
            copy.wait()
        arrived(rows.at[c, pl.ds(0, PLANE - 1)], d_recv.at[c])
        slot = c % SLOTS
        got = rows[c].reshape(PLANE * spots, width)
        if way is aside:
            got = reorder(got)
        acc_gate[...] += jnp.dot(got, w_gate[slot], preferred_element_type=jnp.float32)
        acc_up[...] += jnp.dot(got, w_up[slot], preferred_element_type=jnp.float32)

        @pl.when(c + SLOTS < chunks)
        def _():
            for copy in load_in(c + SLOTS):
                copy.start()

    def step(c, carry):
        pl.when(c < straight)(lambda: dispatch(ahead, c))
        pl.when(c >= LAG)(lambda: consume(ahead, c - LAG))
        return carry

    lax.fori_loop(0, LAG, step, 0)

    acc_gate[...] = jnp.zeros(acc_gate.shape, jnp.float32)
    acc_up[...] = jnp.zeros(acc_up.shape, jnp.float32)
    if flipped:
        arrived(notes_f.at[pl.ds(0, QUADS - 1)], f_recv)
        expert = lax.div(index, 2) * PLANE + quad * 2 + lax.rem(index, 2)
        spot_f, share_f = prepare(aside, expert.astype(jnp.float32))
        for c in range(straight, chunks):
            dispatch(aside, c)
        weigh(aside, spot_f, share_f)
        size = perm.shape[0]
        held = spots // planes
        row = lax.broadcasted_iota(jnp.int32, (size, 128), 0)
        group = lax.div(row, held)
        at_plane, at_core, at_quad = lax.rem(group, planes), lax.rem(lax.div(group, planes), 2), lax.div(group, 2 * planes)
        target = (at_plane * PLANE + at_core * QUADS + at_quad) * held + lax.rem(row, held)
        for at in range(0, size, 128):
            lane = at + lax.broadcasted_iota(jnp.int32, (size, 128), 1)
            block = jnp.where(lane == target, 1.0, 0.0).astype(jnp.bfloat16)
            perm[:, at : min(at + 128, size)] = block[:, : min(128, size - at)]
    weigh(ahead, spot, share)

    lax.fori_loop(LAG, straight + LAG, step, 0)
    for c in range(straight, chunks):
        consume(aside, c)

    gate = acc_gate[...]
    hid[...] = (gate / (1.0 + jnp.exp(-gate)) * acc_up[...]).astype(jnp.bfloat16)

    load_down.wait()

    def compute(way, c):
        sent(packed.at[c, pl.ds(0, PLANE - 1)], d_send.at[c])
        found = jnp.dot(hid[...], w_down[:, cut(c)], preferred_element_type=jnp.float32)
        if way is aside:
            found = jnp.dot(
                perm[...], found.astype(jnp.bfloat16), preferred_element_type=jnp.float32
            )
        packed[c] = found.reshape(packed.shape[1:]).astype(jnp.bfloat16)
        for i in range(1, PLANE):
            answer_copy(way, c, i).start()
        inbox[c, way.scatter_at] = packed[c, way.scatter_at]

    def compute_ahead(c, carry):
        compute(ahead, c)
        return carry

    first = min(2, straight)
    lax.fori_loop(0, first, compute_ahead, 0)
    for c in range(straight, chunks):
        compute(aside, c)
    lax.fori_loop(first, straight, compute_ahead, 0)

    arrived(loads_in.at[pl.ds(0, PLANE - 1)], l_recv)
    loads_in[q] = loads[q]
    load_ref[...] = (jnp.sum(loads_in[...], axis=0) * load_scale)[:1, :1]

    def combine(way, c):
        arrived(inbox.at[c, pl.ds(0, PLANE - 1)], a_recv.at[c])
        total = jnp.zeros((depth, width), jnp.float32)
        for k in range(PLANE):
            for half in range(2):
                total += jnp.dot(
                    way.shares[k, half], inbox[c, k], preferred_element_type=jnp.float32
                )
        column[c] = total.reshape(column.shape[1:]).astype(jnp.bfloat16)
        for i in range(1, planes):
            sum_copy(way, c, i).start()
        sums_in[c, way.gather_at] = column[c, way.gather_at]

    def combine_ahead(c, carry):
        combine(ahead, c)
        return carry

    lax.fori_loop(0, straight, combine_ahead, 0)
    for c in range(straight, chunks):
        combine(aside, c)

    def gather_sums(c, carry):
        arrived(sums_in.at[c, pl.ds(0, planes - 1)], s_recv.at[c])
        total = sums_in[c, 0].astype(jnp.float32)
        for k in range(1, planes):
            total += sums_in[c, k].astype(jnp.float32)
        out_ref[:, cut(c)] = total.astype(jnp.bfloat16)
        return carry

    lax.fori_loop(0, chunks, gather_sums, 0)

    sent(notes.at[pl.ds(0, planes - 1)], n_send)
    if flipped:
        sent(notes_f.at[pl.ds(0, QUADS - 1)], f_send)
    sent(loads.at[pl.ds(0, PLANE - 1)], l_send)
    sent(column.at[:, pl.ds(0, planes - 1)], x_send)
    sent(column.at[:, pl.ds(0, planes - 1)], s_send)
    sent(packed.at[:, pl.ds(0, PLANE - 1)], a_send)


def layer(x, ids, scores, gate, up, down, devices, tok_mb, capacity, load_scale):
    planes = devices // PLANE
    tokens, model_width = x.shape
    inner = gate.shape[1]
    width = next(w for w in (256, 128) if model_width % w == 0)
    chunks = model_width // width
    spots = planes * (tokens // tok_mb) * capacity
    flipped = FLIPPED if planes == QUADS else 0
    few = (lambda *shape: shape) if flipped else (lambda *shape: (1,) * len(shape))
    dma = pltpu.SemaphoreType.DMA
    vmem = pl.BlockSpec(memory_space=pltpu.VMEM)
    hbm = pl.BlockSpec(memory_space=pl.ANY)
    bf16, f32 = jnp.bfloat16, jnp.float32
    return pl.pallas_call(
        functools.partial(layer_kernel, planes, capacity, tok_mb, load_scale, flipped),
        out_shape=(
            jax.ShapeDtypeStruct((tokens, model_width), bf16),
            jax.ShapeDtypeStruct((1, 1), f32),
        ),
        in_specs=[hbm, vmem, vmem, hbm, hbm, hbm],
        out_specs=(vmem, vmem),
        scratch_shapes=[
            pltpu.VMEM((tokens, model_width), bf16),
            pltpu.VMEM((planes, tokens // tok_mb, 2, ids.shape[1], 128), f32),
            pltpu.VMEM((chunks, planes, tokens, width), bf16),
            pltpu.VMEM((PLANE, spots, planes * tokens), bf16),
            pltpu.VMEM((PLANE, 2, planes * tokens, spots), bf16),
            pltpu.VMEM(few(planes, tokens // tok_mb, 2, ids.shape[1], 128), f32),
            pltpu.VMEM(few(PLANE, spots, planes * tokens), bf16),
            pltpu.VMEM(few(PLANE, 2, planes * tokens, spots), bf16),
            pltpu.VMEM(few(PLANE * spots, PLANE * spots), bf16),
            pltpu.VMEM((chunks, PLANE, spots, width), bf16),
            pltpu.VMEM((chunks, PLANE, spots, width), bf16),
            pltpu.VMEM((PLANE, 8, 128), f32),
            pltpu.VMEM((PLANE, 8, 128), f32),
            pltpu.VMEM((SLOTS, width, inner), bf16),
            pltpu.VMEM((SLOTS, width, inner), bf16),
            pltpu.VMEM((inner, model_width), bf16),
            pltpu.VMEM((PLANE * spots, inner), f32),
            pltpu.VMEM((PLANE * spots, inner), f32),
            pltpu.VMEM((PLANE * spots, inner), bf16),
            pltpu.VMEM((chunks, PLANE, spots, width), bf16),
            pltpu.VMEM((chunks, planes, tokens, width), bf16),
            dma,
            dma((SLOTS,)),
            dma((SLOTS,)),
            dma,
            dma,
            dma,
            dma,
            dma,
            dma,
            dma((chunks,)),
            dma,
            dma,
            dma((chunks,)),
            dma((chunks,)),
            dma,
            dma((chunks,)),
            dma,
            dma((chunks,)),
        ],
        compiler_params=pltpu.CompilerParams(
            collective_id=0, has_side_effects=True, vmem_limit_bytes=66 * 1000 * 1000
        ),
    )(x, ids, scores, gate, up, down)


def shards(hidden, expert_ids, gate_scores, w_gate, w_up, w_down):
    devices = lax.axis_size("ep")
    micro_count, tok_mb, model_width = hidden.shape
    chosen = expert_ids.shape[2]
    capacity = tok_mb * chosen // devices + 1
    tokens = micro_count * tok_mb
    mixed, expert_load = layer(
        hidden.reshape(tokens, model_width),
        expert_ids.transpose(0, 2, 1),
        gate_scores.transpose(0, 2, 1),
        w_gate[0],
        w_up[0],
        w_down[0],
        devices,
        tok_mb,
        capacity,
        devices / (route_scale * tokens * devices),
    )
    return (mixed.reshape(micro_count, tok_mb, model_width), expert_load.reshape(1))


def solution(mesh):
    placed = (
        P(None, "ep", None),
        P(None, "ep", None),
        P(None, "ep", None),
        P("ep", None, None),
        P("ep", None, None),
        P("ep", None, None),
    )
    return jax.shard_map(
        shards,
        mesh=mesh,
        in_specs=placed,
        out_specs=(P(None, "ep", None), P("ep")),
        check_vma=False,
    )
```

time: 123 us -> 119 us (0.967)
  Pallas kernels: 119 us -> 114 us
    pallas_call x1, Pallas kernels: 119 us -> 114 us  [layer(): pl.pallas_call(functools.partial(layer_kernel, planes, capacity, tok_mb,...]
where the time goes in v4:
time: 119 us; the launch traced here: 118 us
  Pallas kernels  114 us (96%)
  between operations  2.46 us (2%)
  local copies, waits for them, and re-layouts  1.82 us (2%)
    pallas_call x1, Pallas kernels, layer(): pl.pallas_call(functools.partial(layer_kernel, planes, capacity, tok_mb,...  114 us

profile of v4, /device:TPU:0, one launch (start us, length us, event | category | flops | bytes accessed | tf_op | source)
XLA Modules:
  0.0 118.4 jit_solution(17791840874954174396)
XLA Ops:
  0.6 114.1 %shard_map.77 = (bf16[64,3584]{1,0:T(8,128)(2,1)}, f32[1,1]{1,0:T(1,128)}) custom-call(bf16[64,3584]{1,0:T(8,128)(2,1)} %bitcast.12, s32[2,8,32]{2,1,0:T(8,128)} %bitcast.13, f32[2,8,32]{2,1,0:T(8,128)} %bitcast.14, bf16[3584,1024]{1,0:T(8,128)(2,1)} %bitcast.8, bf16[3584,1024]{1,0:T(8,128)(2,1)} %bitcast.9, bf16[1024,3584]{1,0:T(8,128)(2,1)} %bitcast.10), custom_call_target="tpu_custom_call" | custom-call | tf_op jit(solution)/shard_map/pallas_call | solution.py:436
  114.7 1.8 %copy.10 = bf16[2,32,3584]{2,1,0:T(8,128)(2,1)} copy(bf16[2,32,3584]{2,1,0:T(8,128)(2,1)} %bitcast.11) | data formatting | bytes 917504

commit v5 on v4

--- a/solution.py
+++ b/solution.py
@@ -11,6 +11,8 @@
 PLANE = 8
 SLOTS = 3
 LAG = 3
+AHEAD = 3
+ASIDE = (5, 8)
 QUADS = PLANE // 2
 FLIPPED = 2
 MESH = pl.DeviceIdType.MESH
@@ -73,6 +75,8 @@
     n_recv,
     f_send,
     f_recv,
+    x_far,
+    s_far,
     x_send,
     x_recv,
     l_send,
@@ -132,6 +136,10 @@
         shares_f,
     )
 
+    near = p + 1 - 2 * (p % 2)
+    far = (p + 2) % planes
+    last = (near + 2) % planes
+
     barrier = pltpu.get_barrier_semaphore()
 
     def greet(other):
@@ -197,6 +205,30 @@
         place = sums_in.at[c, way.gather_at]
         return remote(column.at[c, at], place, s_send, s_recv.at[c], other)
 
+    def column_dev(at):
+        return at * PLANE + q
+
+    def x_first(c):
+        place = column.at[c, p]
+        mine = x_ref.at[:, cut(c)]
+        return (
+            remote(mine, place, x_send, x_recv.at[c], column_dev(near)),
+            remote(mine, place, x_send, x_far.at[c], column_dev(far)),
+        )
+
+    def x_relay(c):
+        place = column.at[c, far]
+        return remote(place, place, x_send, x_recv.at[c], column_dev(near))
+
+    def sum_first(c):
+        return tuple(
+            remote(column.at[c, at], sums_in.at[c, k], s_send, s_recv.at[c], column_dev(near))
+            for k, at in enumerate((near, last))
+        )
+
+    def sum_relay(c):
+        return remote(sums_in.at[c, 3], sums_in.at[c, 2], s_send, s_far.at[c], column_dev(far))
+
     def arrived(ref, sem):
         remote(ref, ref, sem, sem, ahead.scatter_of(1)[1]).wait_recv()
 
@@ -212,15 +244,24 @@
         column[c, way.gather_at] = x_ref[:, cut(c)]
 
     def send_ahead(c, carry):
-        send_x(ahead, c)
+        if flipped:
+            for copy in x_first(c):
+                copy.start()
+            column[c, p] = x_ref[:, cut(c)]
+        else:
+            send_x(ahead, c)
         return carry
+
+    def relay_x(c):
+        arrived(column.at[c, pl.ds(0, 1)], x_far.at[c])
+        x_relay(c).start()
 
     if flipped:
         for i in range(1, QUADS):
             notes_copy(aside, i, f_send, f_recv).start()
         for c in range(straight, chunks):
             send_x(aside, c)
-    lax.fori_loop(0, straight, send_ahead, 0)
+    lax.fori_loop(0, min(2, straight) if flipped else straight, send_ahead, 0)
 
     load_down.start()
     arrived(notes.at[pl.ds(0, planes - 1)], n_recv)
@@ -286,7 +327,8 @@
         loads_copy(i).start()
 
     def dispatch(way, c):
-        arrived(column.at[c, pl.ds(0, planes - 1)], x_recv.at[c])
+        count = planes - 2 if flipped and way is ahead else planes - 1
+        arrived(column.at[c, pl.ds(0, count)], x_recv.at[c])
         tokens_here = column[c].reshape(depth, width)
         found = jnp.dot(
             way.picks[...].reshape(PLANE * spots, depth),
@@ -317,11 +359,26 @@
             for copy in load_in(c + SLOTS):
                 copy.start()
 
+    def relay_and_send(c):
+        relay_x(c)
+
+        @pl.when(c + 2 < straight)
+        def _():
+            send_ahead(c + 2, 0)
+
     def step(c, carry):
         pl.when(c < straight)(lambda: dispatch(ahead, c))
+        if flipped:
+            pl.when(c + AHEAD < straight)(lambda: relay_and_send(c + AHEAD))
+            for k in range(flipped):
+                pl.when(c == ASIDE[k])(lambda k=k: dispatch(aside, straight + k))
         pl.when(c >= LAG)(lambda: consume(ahead, c - LAG))
         return carry
 
+    if flipped:
+        for c in range(AHEAD):
+            relay_x(c)
+            send_ahead(c + 2, 0)
     lax.fori_loop(0, LAG, step, 0)
 
     acc_gate[...] = jnp.zeros(acc_gate.shape, jnp.float32)
@@ -330,8 +387,6 @@
         arrived(notes_f.at[pl.ds(0, QUADS - 1)], f_recv)
         expert = lax.div(index, 2) * PLANE + quad * 2 + lax.rem(index, 2)
         spot_f, share_f = prepare(aside, expert.astype(jnp.float32))
-        for c in range(straight, chunks):
-            dispatch(aside, c)
         weigh(aside, spot_f, share_f)
         size = perm.shape[0]
         held = spots // planes
@@ -389,17 +444,41 @@
                     way.shares[k, half], inbox[c, k], preferred_element_type=jnp.float32
                 )
         column[c] = total.reshape(column.shape[1:]).astype(jnp.bfloat16)
-        for i in range(1, planes):
-            sum_copy(way, c, i).start()
-        sums_in[c, way.gather_at] = column[c, way.gather_at]
+        if flipped and way is ahead:
+            for copy in sum_first(c):
+                copy.start()
+        else:
+            for i in range(1, planes):
+                sum_copy(way, c, i).start()
+            sums_in[c, way.gather_at] = column[c, way.gather_at]
+
+    def join(c):
+        arrived(sums_in.at[c, pl.ds(0, 2)], s_recv.at[c])
+        pair = column[c, far].astype(jnp.float32) + sums_in[c, 1].astype(jnp.float32)
+        sums_in[c, 3] = pair.astype(jnp.bfloat16)
+        sum_relay(c).start()
 
     def combine_ahead(c, carry):
         combine(ahead, c)
+        if flipped:
+            pl.when(c >= 1)(lambda: join(c - 1))
         return carry
 
-    lax.fori_loop(0, straight, combine_ahead, 0)
+    sent(column.at[:, pl.ds(0, planes - 1)], x_send)
+    half = straight // 2
+    lax.fori_loop(0, half, combine_ahead, 0)
     for c in range(straight, chunks):
         combine(aside, c)
+    lax.fori_loop(half, straight, combine_ahead, 0)
+    if flipped:
+        join(straight - 1)
+
+    def total_joined(c, carry):
+        arrived(sums_in.at[c, pl.ds(0, 1)], s_far.at[c])
+        total = column[c, p].astype(jnp.float32) + sums_in[c, 0].astype(jnp.float32)
+        total += sums_in[c, 2].astype(jnp.float32)
+        out_ref[:, cut(c)] = total.astype(jnp.bfloat16)
+        return carry
 
     def gather_sums(c, carry):
         arrived(sums_in.at[c, pl.ds(0, planes - 1)], s_recv.at[c])
@@ -409,13 +488,15 @@
         out_ref[:, cut(c)] = total.astype(jnp.bfloat16)
         return carry
 
-    lax.fori_loop(0, chunks, gather_sums, 0)
+    lax.fori_loop(0, straight - 1 if flipped else straight, total_joined if flipped else gather_sums, 0)
+    lax.fori_loop(straight, chunks, gather_sums, 0)
+    if flipped:
+        total_joined(straight - 1, 0)
 
     sent(notes.at[pl.ds(0, planes - 1)], n_send)
     if flipped:
         sent(notes_f.at[pl.ds(0, QUADS - 1)], f_send)
     sent(loads.at[pl.ds(0, PLANE - 1)], l_send)
-    sent(column.at[:, pl.ds(0, planes - 1)], x_send)
     sent(column.at[:, pl.ds(0, planes - 1)], s_send)
     sent(packed.at[:, pl.ds(0, PLANE - 1)], a_send)
 
@@ -471,6 +552,8 @@
             dma,
             dma,
             dma,
+            dma((chunks,)),
+            dma((chunks,)),
             dma,
             dma((chunks,)),
             dma,

time: 119 us -> 112 us (0.941)
  Pallas kernels: 114 us -> 107 us
    pallas_call x1, Pallas kernels: 114 us -> 107 us  [layer(): pl.pallas_call(functools.partial(layer_kernel, planes, capacity, tok_mb,...]
where the time goes in v5:
time: 112 us; the launch traced here: 111 us
  Pallas kernels  107 us (96%)
  between operations  2.46 us (2%)
  local copies, waits for them, and re-layouts  1.82 us (2%)
    pallas_call x1, Pallas kernels, layer(): pl.pallas_call(functools.partial(layer_kernel, planes, capacity, tok_mb,...  107 us

profile of v5, /device:TPU:0, one launch (start us, length us, event | category | flops | bytes accessed | tf_op | source)
XLA Modules:
  0.0 111.3 jit_solution(16667668850783105892)
XLA Ops:
  0.6 107.0 %shard_map.77 = (bf16[64,3584]{1,0:T(8,128)(2,1)}, f32[1,1]{1,0:T(1,128)}) custom-call(bf16[64,3584]{1,0:T(8,128)(2,1)} %bitcast.12, s32[2,8,32]{2,1,0:T(8,128)} %bitcast.13, f32[2,8,32]{2,1,0:T(8,128)} %bitcast.14, bf16[3584,1024]{1,0:T(8,128)(2,1)} %bitcast.8, bf16[3584,1024]{1,0:T(8,128)(2,1)} %bitcast.9, bf16[1024,3584]{1,0:T(8,128)(2,1)} %bitcast.10), custom_call_target="tpu_custom_call" | custom-call | tf_op jit(solution)/shard_map/pallas_call | solution.py:517
  107.7 1.8 %copy.10 = bf16[2,32,3584]{2,1,0:T(8,128)(2,1)} copy(bf16[2,32,3584]{2,1,0:T(8,128)(2,1)} %bitcast.11) | data formatting | bytes 917504

commit v6 on v5

--- a/solution.py
+++ b/solution.py
@@ -10,9 +10,11 @@
 route_scale = 2.5
 PLANE = 8
 SLOTS = 3
-LAG = 3
-AHEAD = 3
+LAG = 4
+AHEAD = 2
 ASIDE = (5, 8)
+FIRST = 1
+MIDDLE = 6
 QUADS = PLANE // 2
 FLIPPED = 2
 MESH = pl.DeviceIdType.MESH
@@ -96,7 +98,19 @@
     micro_count, chosen, _ = ids_ref.shape
     spots = packed.shape[2]
     depth = planes * tokens
-    straight = chunks - flipped
+    turned = tuple(chunks - 2 * flipped + 2 * k for k in range(flipped))
+
+    def is_turned(c):
+        hit = c == turned[0]
+        for at in turned[1:]:
+            hit = hit | (c == at)
+        return hit
+
+    def is_straight(c):
+        good = (c >= 0) & (c < chunks)
+        for at in turned:
+            good = good & (c != at)
+        return good
 
     def cut(c):
         return pl.ds(pl.multiple_of(c * width, width), width)
@@ -112,6 +126,9 @@
 
     hidden_copy = pltpu.make_async_copy(hidden_ref, x_ref, hidden_sem)
     hidden_copy.start()
+
+    def is_joined(c):
+        return is_straight(c) & (c < chunks - 1)
 
     turn = p * 2 + core
     ahead = Route(
@@ -259,9 +276,9 @@
     if flipped:
         for i in range(1, QUADS):
             notes_copy(aside, i, f_send, f_recv).start()
-        for c in range(straight, chunks):
+        for c in turned:
             send_x(aside, c)
-    lax.fori_loop(0, min(2, straight) if flipped else straight, send_ahead, 0)
+    lax.fori_loop(0, 2 if flipped else chunks, send_ahead, 0)
 
     load_down.start()
     arrived(notes.at[pl.ds(0, planes - 1)], n_recv)
@@ -343,7 +360,7 @@
     def reorder(values):
         return jnp.dot(perm[...], values, preferred_element_type=jnp.float32).astype(jnp.bfloat16)
 
-    def consume(way, c):
+    def consume(way, c, final=False):
         for copy in load_in(c):
             copy.wait()
         arrived(rows.at[c, pl.ds(0, PLANE - 1)], d_recv.at[c])
@@ -351,6 +368,17 @@
         got = rows[c].reshape(PLANE * spots, width)
         if way is aside:
             got = reorder(got)
+        if final:
+            for at in range(0, hid.shape[1], 256):
+                tile = slice(at, at + 256)
+                gate = acc_gate[:, tile] + jnp.dot(
+                    got, w_gate[slot, :, tile], preferred_element_type=jnp.float32
+                )
+                upper = acc_up[:, tile] + jnp.dot(
+                    got, w_up[slot, :, tile], preferred_element_type=jnp.float32
+                )
+                hid[:, tile] = (gate / (1.0 + jnp.exp(-gate)) * upper).astype(jnp.bfloat16)
+            return
         acc_gate[...] += jnp.dot(got, w_gate[slot], preferred_element_type=jnp.float32)
         acc_up[...] += jnp.dot(got, w_up[slot], preferred_element_type=jnp.float32)
 
@@ -359,20 +387,19 @@
             for copy in load_in(c + SLOTS):
                 copy.start()
 
-    def relay_and_send(c):
-        relay_x(c)
-
-        @pl.when(c + 2 < straight)
-        def _():
-            send_ahead(c + 2, 0)
-
     def step(c, carry):
-        pl.when(c < straight)(lambda: dispatch(ahead, c))
+        pl.when(is_straight(c))(lambda: dispatch(ahead, c))
         if flipped:
-            pl.when(c + AHEAD < straight)(lambda: relay_and_send(c + AHEAD))
+            pl.when(is_straight(c + AHEAD))(lambda: relay_x(c + AHEAD))
+
+            @pl.when(is_straight(c + AHEAD + 2))
+            def _():
+                send_ahead(c + AHEAD + 2, 0)
+
             for k in range(flipped):
-                pl.when(c == ASIDE[k])(lambda k=k: dispatch(aside, straight + k))
-        pl.when(c >= LAG)(lambda: consume(ahead, c - LAG))
+                pl.when(c == ASIDE[k])(lambda k=k: dispatch(aside, turned[k]))
+            pl.when(is_turned(c - LAG))(lambda: consume(aside, c - LAG))
+        pl.when(is_straight(c - LAG))(lambda: consume(ahead, c - LAG))
         return carry
 
     if flipped:
@@ -400,12 +427,9 @@
             perm[:, at : min(at + 128, size)] = block[:, : min(128, size - at)]
     weigh(ahead, spot, share)
 
-    lax.fori_loop(LAG, straight + LAG, step, 0)
-    for c in range(straight, chunks):
-        consume(aside, c)
-
-    gate = acc_gate[...]
-    hid[...] = (gate / (1.0 + jnp.exp(-gate)) * acc_up[...]).astype(jnp.bfloat16)
+    lax.fori_loop(LAG, chunks + LAG - 1, step, 0)
+    consume(ahead, chunks - 1, True)
+
 
     load_down.wait()
 
@@ -422,20 +446,18 @@
         inbox[c, way.scatter_at] = packed[c, way.scatter_at]
 
     def compute_ahead(c, carry):
-        compute(ahead, c)
+        pl.when(is_straight(c))(lambda: compute(ahead, c))
+        for k in range(flipped):
+            pl.when(c == FIRST + k)(lambda k=k: compute(aside, turned[k]))
         return carry
 
-    first = min(2, straight)
-    lax.fori_loop(0, first, compute_ahead, 0)
-    for c in range(straight, chunks):
-        compute(aside, c)
-    lax.fori_loop(first, straight, compute_ahead, 0)
+    lax.fori_loop(0, chunks, compute_ahead, 0)
 
     arrived(loads_in.at[pl.ds(0, PLANE - 1)], l_recv)
     loads_in[q] = loads[q]
     load_ref[...] = (jnp.sum(loads_in[...], axis=0) * load_scale)[:1, :1]
 
-    def combine(way, c):
+    def combine(way, c, joined=False):
         arrived(inbox.at[c, pl.ds(0, PLANE - 1)], a_recv.at[c])
         total = jnp.zeros((depth, width), jnp.float32)
         for k in range(PLANE):
@@ -444,7 +466,7 @@
                     way.shares[k, half], inbox[c, k], preferred_element_type=jnp.float32
                 )
         column[c] = total.reshape(column.shape[1:]).astype(jnp.bfloat16)
-        if flipped and way is ahead:
+        if joined:
             for copy in sum_first(c):
                 copy.start()
         else:
@@ -459,39 +481,41 @@
         sum_relay(c).start()
 
     def combine_ahead(c, carry):
-        combine(ahead, c)
         if flipped:
-            pl.when(c >= 1)(lambda: join(c - 1))
+            pl.when(is_joined(c))(lambda: combine(ahead, c, True))
+            pl.when(c == chunks - 1)(lambda: combine(ahead, c))
+            pl.when(is_joined(c - 1))(lambda: join(c - 1))
+            for k in range(flipped):
+                pl.when(c == MIDDLE + k)(lambda k=k: combine(aside, turned[k]))
+        else:
+            combine(ahead, c)
         return carry
 
     sent(column.at[:, pl.ds(0, planes - 1)], x_send)
-    half = straight // 2
-    lax.fori_loop(0, half, combine_ahead, 0)
-    for c in range(straight, chunks):
-        combine(aside, c)
-    lax.fori_loop(half, straight, combine_ahead, 0)
-    if flipped:
-        join(straight - 1)
-
-    def total_joined(c, carry):
+    lax.fori_loop(0, chunks, combine_ahead, 0)
+
+    def total_joined(c):
         arrived(sums_in.at[c, pl.ds(0, 1)], s_far.at[c])
         total = column[c, p].astype(jnp.float32) + sums_in[c, 0].astype(jnp.float32)
         total += sums_in[c, 2].astype(jnp.float32)
         out_ref[:, cut(c)] = total.astype(jnp.bfloat16)
-        return carry
-
-    def gather_sums(c, carry):
+
+    def gather_sums(c):
         arrived(sums_in.at[c, pl.ds(0, planes - 1)], s_recv.at[c])
         total = sums_in[c, 0].astype(jnp.float32)
         for k in range(1, planes):
             total += sums_in[c, k].astype(jnp.float32)
         out_ref[:, cut(c)] = total.astype(jnp.bfloat16)
+
+    def finish(c, carry):
+        if flipped:
+            pl.when(is_turned(c) | (c == chunks - 1))(lambda: gather_sums(c))
+            pl.when(is_joined(c))(lambda: total_joined(c))
+        else:
+            gather_sums(c)
         return carry
 
-    lax.fori_loop(0, straight - 1 if flipped else straight, total_joined if flipped else gather_sums, 0)
-    lax.fori_loop(straight, chunks, gather_sums, 0)
-    if flipped:
-        total_joined(straight - 1, 0)
+    lax.fori_loop(0, chunks, finish, 0)
 
     sent(notes.at[pl.ds(0, planes - 1)], n_send)
     if flipped:

time: 112 us -> 109 us (0.973)
  Pallas kernels: 107 us -> 105 us
    pallas_call x1, Pallas kernels: 107 us -> 105 us  [layer(): pl.pallas_call(functools.partial(layer_kernel, planes, capacity, tok_mb,...]
where the time goes in v6:
time: 109 us
  Pallas kernels  105 us (96%)
  between operations  2.46 us (2%)
  local copies, waits for them, and re-layouts  1.82 us (2%)
    pallas_call x1, Pallas kernels, layer(): pl.pallas_call(functools.partial(layer_kernel, planes, capacity, tok_mb,...  105 us

profile of v6, /device:TPU:0, one launch (start us, length us, event | category | flops | bytes accessed | tf_op | source)
XLA Modules:
  0.0 109.0 jit_solution(1503166933236953527)
XLA Ops:
  0.6 104.7 %shard_map.77 = (bf16[64,3584]{1,0:T(8,128)(2,1)}, f32[1,1]{1,0:T(1,128)}) custom-call(bf16[64,3584]{1,0:T(8,128)(2,1)} %bitcast.12, s32[2,8,32]{2,1,0:T(8,128)} %bitcast.13, f32[2,8,32]{2,1,0:T(8,128)} %bitcast.14, bf16[3584,1024]{1,0:T(8,128)(2,1)} %bitcast.8, bf16[3584,1024]{1,0:T(8,128)(2,1)} %bitcast.9, bf16[1024,3584]{1,0:T(8,128)(2,1)} %bitcast.10), custom_call_target="tpu_custom_call" | custom-call | tf_op jit(solution)/shard_map/pallas_call | solution.py:541
  105.3 1.8 %copy.10 = bf16[2,32,3584]{2,1,0:T(8,128)(2,1)} copy(bf16[2,32,3584]{2,1,0:T(8,128)(2,1)} %bitcast.11) | data formatting | bytes 917504

commit v7 on v6

--- a/solution.py
+++ b/solution.py
@@ -16,6 +16,7 @@
 FIRST = 1
 MIDDLE = 6
 QUADS = PLANE // 2
+ORDER = ((1, 1, 0), (1, 1, 1), (0, 1, 0), (1, 0, 0), (0, 1, 1), (1, 0, 1), (0, 0, 1))
 FLIPPED = 2
 MESH = pl.DeviceIdType.MESH
 
@@ -130,12 +131,17 @@
     def is_joined(c):
         return is_straight(c) & (c < chunks - 1)
 
+    def beside(i):
+        y, x, c = ORDER[i - 1]
+        at = (q // 4 + y) % 2 * 4 + (quad + x) % 2 * 2 + (core + c) % 2
+        return at, p * PLANE + at
+
     turn = p * 2 + core
     ahead = Route(
         p,
         lambda i: ((p + i) % planes, ((p + i) % planes) * PLANE + q),
         q,
-        lambda i: ((q + i) % PLANE, p * PLANE + (q + i) % PLANE),
+        beside,
         notes,
         picks,
         shares,

time: 109 us -> 110 us (level)
  no operation moved by 1% of the time
where the time goes in v7:
time: 110 us; the launch traced here: 109 us
  Pallas kernels  105 us (95%)
  between operations  2.46 us (2%)
  local copies, waits for them, and re-layouts  1.82 us (2%)
    pallas_call x1, Pallas kernels, layer(): pl.pallas_call(functools.partial(layer_kernel, planes, capacity, tok_mb,...  105 us

profile of v7, /device:TPU:0, one launch (start us, length us, event | category | flops | bytes accessed | tf_op | source)
XLA Modules:
  0.0 109.4 jit_solution(17422865238528439923)
XLA Ops:
  0.6 105.2 %shard_map.77 = (bf16[64,3584]{1,0:T(8,128)(2,1)}, f32[1,1]{1,0:T(1,128)}) custom-call(bf16[64,3584]{1,0:T(8,128)(2,1)} %bitcast.12, s32[2,8,32]{2,1,0:T(8,128)} %bitcast.13, f32[2,8,32]{2,1,0:T(8,128)} %bitcast.14, bf16[3584,1024]{1,0:T(8,128)(2,1)} %bitcast.8, bf16[3584,1024]{1,0:T(8,128)(2,1)} %bitcast.9, bf16[1024,3584]{1,0:T(8,128)(2,1)} %bitcast.10), custom_call_target="tpu_custom_call" | custom-call | tf_op jit(solution)/shard_map/pallas_call | solution.py:547
  105.8 1.8 %copy.10 = bf16[2,32,3584]{2,1,0:T(8,128)(2,1)} copy(bf16[2,32,3584]{2,1,0:T(8,128)(2,1)} %bitcast.11) | data formatting | bytes 917504
